TPU v7x, 32 devices: a whole 2x2x4 slice. The times are simulated.
32 devices in a mesh: data: 32 (over z, y, x, core).
Axes of the slice: x: 2, y: 2, z: 4, core: 2. Of those that a mesh axis runs over, the one named last changes fastest.
Arguments:
- feat_a: bfloat16 [2048, 2048], P('data')
- feat_b: bfloat16 [2048, 2048], P('data')
- w_one: bfloat16 [2048, 2048], replicated
- w_two: bfloat16 [2048, 2048], replicated
- w_three: bfloat16 [2048, 2048], replicated
- g_one: float32 [2048], replicated
- b_one: float32 [2048], replicated
- g_two: float32 [2048], replicated
- b_two: float32 [2048], replicated
- lam_off: float32 [], replicated
Outputs:
- output 1: float32 [], replicated
- output 2: float32 [2048, 2048], replicated
- output 3: float32 [2048, 2048], replicated
- output 4: float32 [2048, 2048], replicated
- output 5: float32 [2048], replicated
- output 6: float32 [2048], replicated
- output 7: float32 [2048], replicated
- output 8: float32 [2048], replicated
All inputs are finite; a program needn't handle non-finite values.
Results may differ from a plain program's by a relative error of at most 0.00637.
Values are sent between devices in bfloat16 or wider.
A program may use at most 1 GiB of HBM per device.

v0:
```python
import jax
import jax.numpy as jnp
from jax import lax
from jax.sharding import PartitionSpec as P

NORM_EPS = 1e-5
BATCH_AXIS = 'data'


def global_norm(pre, rows_all):
    stat_sums = lax.psum(jnp.stack([jnp.sum(pre, axis=1), jnp.sum(pre * pre, axis=1)]), BATCH_AXIS)
    mean_val = stat_sums[0] / rows_all
    var_val = stat_sums[1] / rows_all - mean_val * mean_val
    inv_std = lax.rsqrt(var_val + NORM_EPS)[:, None, :]
    return (pre - mean_val[:, None, :]) * inv_std, inv_std


def global_norm_back(grad_norm, normed, inv_std, rows_all):
    stat_sums = lax.psum(jnp.stack([jnp.sum(grad_norm, axis=1), jnp.sum(grad_norm * normed, axis=1)]), BATCH_AXIS)
    mean_grad = (stat_sums[0] / rows_all)[:, None, :]
    mean_cross = (stat_sums[1] / rows_all)[:, None, :]
    return inv_std * (grad_norm - mean_grad - normed * mean_cross)


def corr_loss(corr, lam_off, width):
    diag_c = jnp.diagonal(corr)
    loss_val = jnp.sum((1.0 - diag_c) ** 2) + lam_off * (jnp.sum(corr * corr) - jnp.sum(diag_c * diag_c))
    on_diag = jnp.arange(width)[:, None] == jnp.arange(width)[None, :]
    grad_c = jnp.where(on_diag, -2.0 * (1.0 - corr), 2.0 * lam_off * corr).astype(jnp.bfloat16)
    return loss_val, grad_c


def solution(mesh):
    num_devs = mesh.shape[BATCH_AXIS]

    def local_step(feat_a, feat_b, w_one, w_two, w_three, g_one, b_one, g_two, b_two, lam_off):
        rows_all = feat_a.shape[0] * num_devs
        width = w_two.shape[0]
        features = jnp.stack([feat_a, feat_b])
        pre_one = jnp.einsum('vnf,fd->vnd', features, w_one, preferred_element_type=jnp.float32)
        norm_one, inv_one = global_norm(pre_one, rows_all)
        aff_one = norm_one * g_one + b_one
        act_one = jnp.maximum(aff_one, 0.0).astype(jnp.bfloat16)
        pre_two = jnp.einsum('woe,ef->wof', act_one, w_two, preferred_element_type=jnp.float32)
        norm_two, inv_two = global_norm(pre_two, rows_all)
        aff_two = norm_two * g_two + b_two
        act_two = jnp.maximum(aff_two, 0.0).astype(jnp.bfloat16)
        proj_out = jnp.einsum('woe,ef->wof', act_two, w_three, preferred_element_type=jnp.float32)
        norm_out, inv_out = global_norm(proj_out, rows_all)
        emb = norm_out.astype(jnp.bfloat16)
        part_corr = jnp.einsum('nd,ne->de', emb[0], emb[1], preferred_element_type=jnp.float32)
        corr = lax.psum(part_corr, BATCH_AXIS) / rows_all
        loss_val, grad_c = corr_loss(corr, lam_off, width)
        grad_a = jnp.einsum('ne,de->nd', emb[1], grad_c, preferred_element_type=jnp.float32)
        grad_b = jnp.einsum('nd,de->ne', emb[0], grad_c, preferred_element_type=jnp.float32)
        grad_emb = jnp.stack([grad_a, grad_b]) / rows_all
        grad_proj = global_norm_back(grad_emb, norm_out, inv_out, rows_all).astype(jnp.bfloat16)
        dw_three = jnp.einsum('woe,wof->ef', act_two, grad_proj, preferred_element_type=jnp.float32)
        grad_act_two = jnp.einsum('wof,ef->woe', grad_proj, w_three, preferred_element_type=jnp.float32)
        grad_aff_two = jnp.where(aff_two > 0, grad_act_two, 0.0)
        dg_two = jnp.sum(grad_aff_two * norm_two, axis=(0, 1))
        db_two = jnp.sum(grad_aff_two, axis=(0, 1))
        grad_pre_two = global_norm_back(grad_aff_two * g_two, norm_two, inv_two, rows_all).astype(jnp.bfloat16)
        dw_two = jnp.einsum('woe,wof->ef', act_one, grad_pre_two, preferred_element_type=jnp.float32)
        grad_act_one = jnp.einsum('wof,ef->woe', grad_pre_two, w_two, preferred_element_type=jnp.float32)
        grad_aff_one = jnp.where(aff_one > 0, grad_act_one, 0.0)
        dg_one = jnp.sum(grad_aff_one * norm_one, axis=(0, 1))
        db_one = jnp.sum(grad_aff_one, axis=(0, 1))
        grad_pre_one = global_norm_back(grad_aff_one * g_one, norm_one, inv_one, rows_all).astype(jnp.bfloat16)
        dw_one = jnp.einsum('vnf,vnd->fd', features, grad_pre_one, preferred_element_type=jnp.float32)
        totals = lax.psum((dw_one, dw_two, dw_three, dg_one, db_one, dg_two, db_two), BATCH_AXIS)
        return (loss_val,) + tuple(totals)

    row_spec = P(BATCH_AXIS, None)
    return jax.shard_map(local_step, mesh=mesh, in_specs=(row_spec, row_spec, P(), P(), P(), P(), P(), P(), P(), P()), out_specs=(P(), P(), P(), P(), P(), P(), P(), P()), check_vma=False)
```

profile of v0, /device:TPU:0, one launch (start us, length us, event | category | flops | bytes accessed | tf_op | source)
XLA Modules:
  0.0 1459.2 jit_solution(14487206972879985069)
XLA Ops:
  7.2 4.9 fusion.49
  12.2 42.1 %psum.98 = f32[2,2,2048]{2,1,0:T(2,128)S(1)} all-reduce(f32[2,2,2048]{2,1,0:T(2,128)S(1)} %pad_maximum_fusion.3), channel_id=1, replica_groups=mesh['data'=32] {'data'}, use_global_device_ids=true, to_apply=%region_2.0 | all-reduce | flops 8192 | bytes 65536 | tf_op jit(solution)/shard_map/psum | solution.py:11
  54.3 4.8 fusion.48
  59.2 40.4 %psum.99 = f32[2,2,2048]{2,1,0:T(2,128)S(1)} all-reduce(f32[2,2,2048]{2,1,0:T(2,128)S(1)} %pad_maximum_fusion.4), channel_id=1, replica_groups=mesh['data'=32] {'data'}, use_global_device_ids=true, to_apply=%region_5.0 | all-reduce | flops 8192 | bytes 65536 | tf_op jit(solution)/shard_map/psum | solution.py:11
  99.6 4.8 fusion.47
  104.4 39.8 %psum.100 = f32[2,2,2048]{2,1,0:T(2,128)S(1)} all-reduce(f32[2,2,2048]{2,1,0:T(2,128)S(1)} %pad_maximum_fusion.5), channel_id=1, replica_groups=mesh['data'=32] {'data'}, use_global_device_ids=true, to_apply=%region_8.0 | all-reduce | flops 8192 | bytes 65536 | tf_op jit(solution)/shard_map/psum | solution.py:11
  145.2 8.5 fusion.23
  154.7 277.2 %all-reduce.6.cloned.1.call-done = f32[2048,2048]{1,0:T(8,128)} async-done(((f32[2048,2048]{1,0:T(8,128)}), f32[2048,2048]{1,0:T(8,128)}) %all-reduce.6.cloned.1.call-update) | async-done | bytes 16777232 | tf_op jit(solution)/shard_map/psum | solution.py:52
  431.8 10.0 convolution_bitcast_fusion.4
  445.4 40.4 %psum.102 = f32[2,2,2048]{2,1,0:T(2,128)S(1)} all-reduce(f32[2,2,2048]{2,1,0:T(2,128)S(1)} %pad_maximum_fusion.6), channel_id=1, replica_groups=mesh['data'=32] {'data'}, use_global_device_ids=true, to_apply=%region_15.16 | all-reduce | flops 8192 | bytes 65536 | tf_op jit(solution)/shard_map/psum | solution.py:19
  487.3 8.1 multiply_reduce_fusion.1
  495.4 8.1 convolution_bitcast_fusion
  503.5 39.4 %psum.103 = f32[2,2,2048]{2,1,0:T(2,128)S(1)} all-reduce(f32[2,2,2048]{2,1,0:T(2,128)S(1)} %pad_maximum_fusion.7), channel_id=1, replica_groups=mesh['data'=32] {'data'}, use_global_device_ids=true, to_apply=%region_18.19 | all-reduce | flops 8192 | bytes 65536 | tf_op jit(solution)/shard_map/psum | solution.py:19
  544.5 8.2 multiply_reduce_fusion.2
  553.4 8.5 convolution_bitcast_fusion.1
  561.9 122.1 %all-reduce.8.cloned.1.call-done = (f32[2,2,2048]{2,1,0:T(2,128)}, f32[2048]{0:T(1024)}, f32[2048]{0:T(1024)}, f32[2048]{0:T(1024)}, f32[2048]{0:T(1024)}) async-done(((f32[2,2,2048]{2,1,0:T(2,128)}, f32[2048]{0:T(1024)}, f32[2048]{0:T(1024)}, f32[2048]{0:T(1024)}, f32[2048]{0:T(1024)}), (f32[2,2,2048]{2,1,0:T(2,128)}, f32[2048]{0:T(1024)}, f32[2048]{0:T(1024)}, f32[2048]{0:T(1024)}, ...) | async-done | bytes 65552 | tf_op jit(solution)/shard_map/psum | solution.py:19
  684.8 9.8 convolution_bitcast_fusion.2
  694.6 13.5 multiply_reduce_fusion
  708.1 33.2 %gather_fusion = f32[2048]{0:T(1024)S(1)} fusion(f32[2048,2048]{1,0:T(8,128)} %get-tuple-element.35, s32[2048]{0:T(1024)S(1)} %bitcast.112), kind=kCustom, calls=%fused_computation | custom fusion | bytes 32768 | tf_op jit(solution)/shard_map/jit(diagonal)/cond/branch_0_fun/gather | solution.py:26
  743.8 671.6 %all-reduce.10.cloned.1.call-done = (f32[2048,2048]{1,0:T(8,128)}, f32[2048,2048]{1,0:T(8,128)}, f32[2048,2048]{1,0:T(8,128)}) async-done(((f32[2048,2048]{1,0:T(8,128)}, f32[2048,2048]{1,0:T(8,128)}, f32[2048,2048]{1,0:T(8,128)}), (f32[2048,2048]{1,0:T(8,128)}, f32[2048,2048]{1,0:T(8,128)}, f32[2048,2048]{1,0:T(8,128)})) %all-reduce.10.cloned.1.call-update) | async-done | bytes 50331664 | tf_op jit(solution)/shard_map/psum | solution.py:71
  1415.5 13.5 copy.28
  1429.0 2.9 copy-done.1
  1431.9 8.5 copy.29
  1443.0 6.2 copy.30
  (72 shorter events, 14.9 us)
Async XLA Ops:
  7.2 92.4 %copy-start.8 = (f32[2048]{0:T(1024)S(1)}, f32[2048]{0:T(1024)}, u32[]{:S(2)}) copy-start(f32[2048]{0:T(1024)} %param.17) | copy-start | bytes 24580
  7.2 92.4 %copy-start.10 = (f32[2048]{0:T(1024)S(1)}, f32[2048]{0:T(1024)}, u32[]{:S(2)}) copy-start(f32[2048]{0:T(1024)} %param.18) | copy-start | bytes 24580
  7.2 424.7 %all-reduce.6.cloned.1.call-start = ((), (), s32[]{:S(2)}) async-start(), calls=%async_computation | async-start | bytes 33554432 | tf_op jit(solution)/shard_map/psum | solution.py:52
  144.4 0.8 copy-start.2
  153.8 530.3 %all-reduce.8.cloned.1.call-start = ((), (), s32[]{:S(2)}) async-start(), calls=%async_computation.1 | async-start | bytes 131072 | tf_op jit(solution)/shard_map/psum | solution.py:19
  431.8 10.6 copy-start
  431.8 10.7 copy-start.3
  442.5 2.0 copy-start.4
  444.6 0.8 copy-start.5
  487.2 57.2 %copy-start.9 = (f32[2048]{0:T(1024)S(1)}, f32[2048]{0:T(1024)}, u32[]{:S(2)}) copy-start(f32[2048]{0:T(1024)} %param.15) | copy-start | bytes 24580
  487.3 57.2 %copy-start.11 = (f32[2048]{0:T(1024)S(1)}, f32[2048]{0:T(1024)}, u32[]{:S(2)}) copy-start(f32[2048]{0:T(1024)} %param.16) | copy-start | bytes 24580
  544.5 140.3 %copy-start.6 = (bf16[64,2048]{1,0:T(8,128)(2,1)S(1)}, bf16[64,2048]{1,0:T(8,128)(2,1)}, u32[]{:S(2)}) copy-start(bf16[64,2048]{1,0:T(8,128)(2,1)} %param.11) | copy-start | bytes 786436
  544.5 140.3 %copy-start.7 = (bf16[64,2048]{1,0:T(8,128)(2,1)S(1)}, bf16[64,2048]{1,0:T(8,128)(2,1)}, u32[]{:S(2)}) copy-start(bf16[64,2048]{1,0:T(8,128)(2,1)} %param.10) | copy-start | bytes 786436
  553.3 862.1 %all-reduce.10.cloned.1.call-start = ((), (), s32[]{:S(2)}) async-start(), calls=%async_computation.2 | async-start | bytes 100663296 | tf_op jit(solution)/shard_map/psum | solution.py:71
  1415.5 16.4 %copy-start.1 = (f32[2048,2048]{1,0:T(8,128)S(1)}, f32[2048,2048]{1,0:T(8,128)}, u32[]{:S(2)}) copy-start(f32[2048,2048]{1,0:T(8,128)} %get-tuple-element.49) | copy-start | bytes 50331652
  1415.5 24.9 %slice-start = ((s8[16777216]{0:T(1024)(128)(4,1)}), s8[4194304]{0:T(1024)(128)(4,1)S(1)}, s32[]{:S(2)}) async-start(s8[16777216]{0:T(1024)(128)(4,1)} %bitcast.113), calls=%async_computation.3 | async-start | bytes 8388608
  1415.5 24.9 %slice-start.1 = ((s8[16777216]{0:T(1024)(128)(4,1)}), s8[4194304]{0:T(1024)(128)(4,1)S(1)}, s32[]{:S(2)}) async-start(s8[16777216]{0:T(1024)(128)(4,1)} %bitcast.113), calls=%async_computation.4 | async-start | bytes 8388608
  1431.9 9.9 slice-start.2
  1431.9 11.1 slice-start.3
  1443.0 6.2 copy-start.15
  1443.0 6.8 copy-start.14
  1443.0 7.4 copy-start.13
  1443.0 8.0 copy-start.12
Sparse Core Ops, SparseCore 0:
  153.9 277.9 all-reduce.5
  553.5 130.5 all-reduce.7
  694.7 720.6 all-reduce.9
where the time goes:
time: 1460 us
  waiting for transfers between devices  1070 us (73%)
  blocking collectives  202 us (14%)
  matrix products  77.8 us (5%)
  local copies, waits for them, and re-layouts  71.2 us (5%)
  other arithmetic  19.1 us (1%)
  between operations  17.8 us (1%)
    psum x1, waiting for transfers between devices, local_step(): lax.psum((dw_one, dw_two, dw_three, dg_one, db_one, dg_two, db_two), BATC...  672 us
    psum x1, waiting for transfers between devices, local_step(): corr = lax.psum(part_corr, BATCH_AXIS) / rows_all  277 us
    psum x3, blocking collectives, global_norm(): lax.psum(jnp.stack([jnp.sum(pre, axis=1), jnp.sum(pre * pre, axis=1)]), B...  122 us
    psum x1, waiting for transfers between devices, global_norm_back(): lax.psum(jnp.stack([jnp.sum(grad_norm, axis=1), jnp.sum(grad_norm * norme...  122 us
    psum x2, blocking collectives, global_norm_back(): lax.psum(jnp.stack([jnp.sum(grad_norm, axis=1), jnp.sum(grad_norm * norme...  79.8 us
    unnamed x47, local copies, waits for them, and re-layouts  38 us
    gather x1, local copies, waits for them, and re-layouts, corr_loss(): diag_c = jnp.diagonal(corr)  33.2 us
  transfers between devices with their start and end apart: 3, of which 3 were waited for; matrix products, arithmetic and copies ran while one was open for 4% of the time, Pallas kernels for 0%

commit v1 on v0

v1 whole, which is shorter than its diff:
```python
import functools

import jax
import jax.numpy as jnp
from jax import lax
from jax.experimental import pallas as pl
from jax.experimental.pallas import tpu as pltpu
from jax.sharding import PartitionSpec as P

NORM_EPS = 1e-5
BATCH_AXIS = 'data'
MESH_ID = pl.DeviceIdType.MESH
TILE = 256
CHUNK = 512
BF = jnp.bfloat16
F32 = jnp.float32


def mm(lhs, rhs, lhs_dim=1, rhs_dim=0):
    return lax.dot_general(lhs, rhs, (((lhs_dim,), (rhs_dim,)), ((), ())), preferred_element_type=F32)


def fold(val):
    return jnp.sum(val.reshape(val.shape[0] // 8, 8, val.shape[1]), axis=0)


def sibling_of(me):
    return me + 1 - 2 * lax.rem(me, 2)


def greet(peers):
    barrier = pltpu.get_barrier_semaphore()
    for peer in peers:
        pl.semaphore_signal(barrier, inc=1, device_id=(peer,), device_id_type=MESH_ID)
    pl.semaphore_wait(barrier, len(peers))


def remote(src, dst, send_sem, recv_sem, dev):
    return pltpu.make_async_remote_copy(src_ref=src, dst_ref=dst, send_sem=send_sem, recv_sem=recv_sem, device_id=(dev,), device_id_type=MESH_ID)


def gather_kernel(rows, own_ref, out_ref, buf, own_sem, sib_s, sib_r, send_sem, recv_sem, half_s, half_r, out_sem):
    me = lax.axis_index(BATCH_AXIS)
    core = lax.rem(me, 2)
    sib = sibling_of(me)
    chip = me // 2
    xpos = lax.rem(chip, 2)
    ypos = lax.rem(chip // 2, 2)
    zpos = chip // 4
    x_dev = me + 2 - 4 * xpos
    y_dev = me + 4 - 8 * ypos
    up_dev = jnp.minimum(zpos + 1, 3) * 8 + lax.rem(me, 8)
    down_dev = jnp.maximum(zpos - 1, 0) * 8 + lax.rem(me, 8)
    barrier = pltpu.get_barrier_semaphore()
    for peer in (sib, x_dev, y_dev):
        pl.semaphore_signal(barrier, inc=1, device_id=(peer,), device_id_type=MESH_ID)
    has_up = zpos < 3
    has_down = zpos > 0

    @pl.when(has_up)
    def _():
        pl.semaphore_signal(barrier, inc=1, device_id=(up_dev,), device_id_type=MESH_ID)

    @pl.when(has_down)
    def _():
        pl.semaphore_signal(barrier, inc=1, device_id=(down_dev,), device_id_type=MESH_ID)
    pl.semaphore_wait(barrier, 3 + (1 - (zpos + 1) // 4) + (zpos + 3) // 4)

    def block(idx):
        return buf.at[pl.ds(pl.multiple_of(idx * 2 * rows, 2 * rows), 2 * rows), :]

    def half(idx, part):
        return buf.at[pl.ds(pl.multiple_of(idx * 2 * rows + part * rows, rows), rows), :]

    own = pltpu.make_async_copy(own_ref.at[core], half(chip, core), own_sem)
    own.start()
    to_sib = remote(own_ref.at[1 - core], half(chip, core), sib_s, sib_r, sib)
    to_sib.start()
    own.wait()
    to_sib.wait()

    def whole(idx, way, dev):
        return remote(block(idx), block(idx), send_sem.at[idx, way], recv_sem.at[idx], dev)

    def part_copy(idx, part, dev):
        return remote(half(idx, part), half(idx, part), half_s.at[idx], half_r.at[idx, part], dev)

    def blk(xx, yy, zz):
        return (zz * 2 + yy) * 2 + xx

    def column(zz, going_up, going_down):
        idx = blk(xpos, ypos, zz)
        whole(idx, 0, x_dev).start()
        whole(idx, 1, y_dev).start()
        if going_up:
            @pl.when(has_up)
            def _():
                whole(idx, 2, up_dev).start()
        if going_down:
            @pl.when(has_down)
            def _():
                whole(idx, 3, down_dev).start()

    def across(zz):
        idx_x = blk(1 - xpos, ypos, zz)
        whole(idx_x, 0, x_dev).wait_recv()
        part_copy(idx_x, 0, y_dev).start()
        idx_y = blk(xpos, 1 - ypos, zz)
        whole(idx_y, 1, y_dev).wait_recv()
        part_copy(idx_y, 1, x_dev).start()

    column(zpos, True, True)
    for dist in range(1, 5):
        for sign in (-1, 1):
            zz = zpos + sign * dist
            if dist < 4:
                @pl.when(jnp.logical_and(zz >= 0, zz < 4))
                def _(zz=zz, sign=sign):
                    whole(blk(xpos, ypos, zz), 0, x_dev).wait_recv()
                    column(zz, sign < 0, sign > 0)
            prev = zpos + sign * (dist - 1)
            if dist > 1 or sign < 0:
                @pl.when(jnp.logical_and(prev >= 0, prev < 4))
                def _(prev=prev):
                    across(prev)
    def finish(zz, carry):
        idx = blk(1 - xpos, 1 - ypos, zz)
        part_copy(idx, 0, y_dev).wait_recv()
        part_copy(idx, 1, x_dev).wait_recv()
        return carry
    lax.fori_loop(0, 4, finish, 0)
    out = pltpu.make_async_copy(buf, out_ref, out_sem)
    out.start()

    def drain(zz, carry):
        col = blk(xpos, ypos, zz)
        whole(col, 0, x_dev).wait_send()
        whole(col, 1, y_dev).wait_send()

        @pl.when(jnp.logical_and(has_up, zz <= zpos))
        def _():
            whole(col, 2, up_dev).wait_send()

        @pl.when(jnp.logical_and(has_down, zz >= zpos))
        def _():
            whole(col, 3, down_dev).wait_send()
        part_copy(blk(1 - xpos, ypos, zz), 0, y_dev).wait_send()
        part_copy(blk(xpos, 1 - ypos, zz), 1, x_dev).wait_send()
        return carry
    lax.fori_loop(0, 4, drain, 0)
    out.wait()


def gather_rows(own, num_devs):
    rows, width = own.shape[1:]
    chips = num_devs // 2
    return pl.pallas_call(
        functools.partial(gather_kernel, rows),
        out_shape=jax.ShapeDtypeStruct((num_devs * rows, width), own.dtype),
        in_specs=[pl.BlockSpec(memory_space=pltpu.VMEM)],
        out_specs=pl.BlockSpec(memory_space=pl.ANY),
        scratch_shapes=[pltpu.VMEM((num_devs * rows, width), own.dtype), pltpu.SemaphoreType.DMA, pltpu.SemaphoreType.DMA, pltpu.SemaphoreType.DMA,
                        pltpu.SemaphoreType.DMA((chips, 4)), pltpu.SemaphoreType.DMA((chips,)),
                        pltpu.SemaphoreType.DMA((chips,)), pltpu.SemaphoreType.DMA((chips, 2)), pltpu.SemaphoreType.DMA],
        compiler_params=pltpu.CompilerParams(collective_id=0, has_side_effects=True, vmem_limit_bytes=60 << 20),
        name='gather_rows',
    )(own)


def pre_stats(x_ref, w, pre_ref):
    rows = x_ref.shape[0]

    def step(i, carry):
        at = pl.ds(pl.multiple_of(i * CHUNK, CHUNK), CHUNK)
        val = mm(x_ref[at, :], w)
        pre_ref[at, :] = val
        return carry[0] + fold(val), carry[1] + fold(val * val)
    zero = jnp.zeros((8, pre_ref.shape[1]), F32)
    tot, sqr = lax.fori_loop(0, rows // CHUNK, step, (zero, zero), unroll=True)
    mean = jnp.sum(tot, axis=0, keepdims=True) / rows
    var = jnp.sum(sqr, axis=0, keepdims=True) / rows - mean * mean
    return mean, lax.rsqrt(var + NORM_EPS)


def layer_kernel(x_ref, w_ref, g_ref, b_ref, act_ref, norm_ref, inv_ref, pre_ref):
    mean, inv = pre_stats(x_ref, w_ref[...], pre_ref)
    inv_ref[...] = inv
    gain, bias = g_ref[...], b_ref[...]

    def fin(i, carry):
        at = pl.ds(pl.multiple_of(i * TILE, TILE), TILE)
        norm = (pre_ref[at, :] - mean) * inv
        norm_ref[at, :] = norm
        act_ref[at, :] = jnp.maximum(norm * gain + bias, 0.0).astype(BF)
        return carry
    lax.fori_loop(0, x_ref.shape[0] // TILE, fin, 0)


def full_spec(shape):
    return pl.BlockSpec(shape, lambda j: (0, 0), pipeline_mode=pl.Buffered(1))


def col_spec(rows):
    return pl.BlockSpec((rows, TILE), lambda j: (0, j))


def row_spec_of(cols):
    return pl.BlockSpec((TILE, cols), lambda j: (j, 0))


def params(limit, **kw):
    return pltpu.CompilerParams(dimension_semantics=('arbitrary',), vmem_limit_bytes=limit << 20, **kw)


def cost(units):
    return pl.CostEstimate(flops=int(units * 2 * 2048 ** 3), bytes_accessed=40 << 20, transcendentals=0)


def layer(x, w, gain, bias):
    rows, width = x.shape[0], w.shape[1]
    return pl.pallas_call(
        layer_kernel, grid=(width // TILE,),
        out_shape=(jax.ShapeDtypeStruct((rows, width), BF), jax.ShapeDtypeStruct((rows, width), F32), jax.ShapeDtypeStruct((1, width), F32)),
        in_specs=[full_spec(x.shape), col_spec(w.shape[0]), col_spec(1), col_spec(1)],
        out_specs=(col_spec(rows), col_spec(rows), col_spec(1)),
        scratch_shapes=[pltpu.VMEM((rows, TILE), F32)],
        compiler_params=params(60), cost_estimate=cost(1), name='layer',
    )(x, w, gain, bias)


def embed_kernel(x_ref, w_ref, emb_ref, norm_ref, inv_ref, other_ref, pre_ref, hold, send_sem, recv_sem):
    j = pl.program_id(0)
    num = pl.num_programs(0)
    me = lax.axis_index(BATCH_AXIS)
    sib = sibling_of(me)

    @pl.when(j == 0)
    def _():
        greet([sib])
    mean, inv = pre_stats(x_ref, w_ref[...], pre_ref)
    inv_ref[...] = inv

    def fin(i, carry):
        at = pl.ds(pl.multiple_of(i * TILE, TILE), TILE)
        norm = (pre_ref[at, :] - mean) * inv
        norm_ref[at, :] = norm
        emb = norm.astype(BF)
        emb_ref[at, :] = emb
        hold[j, at, :] = emb
        return carry
    lax.fori_loop(0, x_ref.shape[0] // TILE, fin, 0)

    def copy(t):
        return remote(hold.at[t], other_ref.at[:, pl.ds(pl.multiple_of(t * TILE, TILE), TILE)], send_sem.at[t], recv_sem.at[t], sib)
    copy(j).start()

    @pl.when(j == num - 1)
    def _():
        def end(t, carry):
            copy(t).wait()
            return carry
        lax.fori_loop(0, num, end, 0)


def embed(x, w):
    rows, width = x.shape[0], w.shape[1]
    tiles = width // TILE
    return pl.pallas_call(
        embed_kernel, grid=(tiles,),
        out_shape=(jax.ShapeDtypeStruct((rows, width), BF), jax.ShapeDtypeStruct((rows, width), F32), jax.ShapeDtypeStruct((1, width), F32), jax.ShapeDtypeStruct((rows, width), BF)),
        in_specs=[full_spec(x.shape), col_spec(w.shape[0])],
        out_specs=(col_spec(rows), col_spec(rows), col_spec(1), pl.BlockSpec(memory_space=pl.ANY)),
        scratch_shapes=[pltpu.VMEM((rows, TILE), F32), pltpu.VMEM((tiles, rows, TILE), BF), pltpu.SemaphoreType.DMA((tiles,)), pltpu.SemaphoreType.DMA((tiles,))],
        compiler_params=params(60, collective_id=1, has_side_effects=True), cost_estimate=cost(1), name='embed',
    )(x, w)


def corr_kernel(lam_ref, emb_ref, other_ref, norm_ref, inv_ref, dout_ref, loss_ref, left, grad_c, scr):
    j = pl.program_id(0)
    rows, width = other_ref.shape
    scale = 1.0 / rows
    lam = lam_ref[0]

    @pl.when(j == 0)
    def _():
        loss_ref[...] = jnp.zeros_like(loss_ref)
    left[...] = emb_ref[...].T

    def corr_step(i, loss):
        at = pl.ds(pl.multiple_of(i * CHUNK, CHUNK), CHUNK)
        corr = mm(left[...], other_ref[:, at]) * scale
        row_id = lax.broadcasted_iota(jnp.int32, corr.shape, 0) + j * TILE
        col_id = lax.broadcasted_iota(jnp.int32, corr.shape, 1) + i * CHUNK
        on_diag = row_id == col_id
        miss = 1.0 - corr
        lam_corr = lam * corr
        grad_c[:, at] = jnp.where(on_diag, -2.0 * miss, 2.0 * lam_corr).astype(BF)
        return loss + fold(jnp.where(on_diag, miss * miss, lam_corr * corr))
    loss = lax.fori_loop(0, width // CHUNK, corr_step, jnp.zeros((8, CHUNK), F32), unroll=True)
    loss_ref[...] += loss

    def emb_step(i, carry):
        at = pl.ds(pl.multiple_of(i * CHUNK, CHUNK), CHUNK)
        val = mm(other_ref[at, :], grad_c[...], 1, 1) * scale
        scr[at, :] = val
        return carry[0] + fold(val), carry[1] + fold(val * norm_ref[at, :])
    zero = jnp.zeros((8, TILE), F32)
    tot, crs = lax.fori_loop(0, rows // CHUNK, emb_step, (zero, zero), unroll=True)
    mean_grad = jnp.sum(tot, axis=0, keepdims=True) / rows
    mean_cross = jnp.sum(crs, axis=0, keepdims=True) / rows
    inv = inv_ref[...]

    def fin(i, carry):
        at = pl.ds(pl.multiple_of(i * TILE, TILE), TILE)
        dout_ref[at, :] = (inv * (scr[at, :] - mean_grad - norm_ref[at, :] * mean_cross)).astype(BF)
        return carry
    lax.fori_loop(0, rows // TILE, fin, 0)


def corr_back(lam_off, emb, other, norm, inv):
    rows, width = emb.shape
    return pl.pallas_call(
        corr_kernel, grid=(width // TILE,),
        out_shape=(jax.ShapeDtypeStruct((rows, width), BF), jax.ShapeDtypeStruct((8, CHUNK), F32)),
        in_specs=[pl.BlockSpec(memory_space=pltpu.SMEM), col_spec(rows), full_spec(other.shape), col_spec(rows), col_spec(1)],
        out_specs=(col_spec(rows), pl.BlockSpec((8, CHUNK), lambda j: (0, 0))),
        scratch_shapes=[pltpu.VMEM((TILE, rows), BF), pltpu.VMEM((TILE, width), BF), pltpu.VMEM((rows, TILE), F32)],
        compiler_params=params(60), cost_estimate=cost(2), name='corr_back',
    )(lam_off.reshape(1), emb, other, norm, inv)


def back_kernel(d_ref, w_ref, norm_ref, inv_ref, g_ref, b_ref, dpre_ref, dg_ref, db_ref, scr):
    rows = d_ref.shape[0]
    gain, bias, inv = g_ref[...], b_ref[...], inv_ref[...]

    def step(i, carry):
        at = pl.ds(pl.multiple_of(i * CHUNK, CHUNK), CHUNK)
        val = mm(d_ref[at, :], w_ref[...], 1, 1)
        norm = norm_ref[at, :]
        val = jnp.where(norm * gain + bias > 0, val, 0.0)
        scr[at, :] = val
        return carry[0] + fold(val), carry[1] + fold(val * norm)
    zero = jnp.zeros((8, TILE), F32)
    tot, crs = lax.fori_loop(0, rows // CHUNK, step, (zero, zero), unroll=True)
    tot = jnp.sum(tot, axis=0, keepdims=True)
    crs = jnp.sum(crs, axis=0, keepdims=True)
    db_ref[...] = tot
    dg_ref[...] = crs
    mean_grad = gain * tot / rows
    mean_cross = gain * crs / rows

    def fin(i, carry):
        at = pl.ds(pl.multiple_of(i * TILE, TILE), TILE)
        dpre_ref[at, :] = (inv * (scr[at, :] * gain - mean_grad - norm_ref[at, :] * mean_cross)).astype(BF)
        return carry
    lax.fori_loop(0, rows // TILE, fin, 0)


def layer_back(grad, w, norm, inv, gain, bias):
    rows, width = norm.shape
    vec = jax.ShapeDtypeStruct((1, width), F32)
    return pl.pallas_call(
        back_kernel, grid=(width // TILE,),
        out_shape=(jax.ShapeDtypeStruct((rows, width), BF), vec, vec),
        in_specs=[full_spec(grad.shape), row_spec_of(w.shape[1]), col_spec(rows), col_spec(1), col_spec(1), col_spec(1)],
        out_specs=(col_spec(rows), col_spec(1), col_spec(1)),
        scratch_shapes=[pltpu.VMEM((rows, TILE), F32)],
        compiler_params=params(60), cost_estimate=cost(1), name='layer_back',
    )(grad, w, norm, inv, gain, bias)


def weights_kernel(acts, grads, small_ref, outs, small_out, lhs, left, rhs, sbuf, rbuf, obuf, small_in, lhs_sem, rhs_sem, ps, pr, os_, or_, ol, ss, sr):
    me = lax.axis_index(BATCH_AXIS)
    core = lax.rem(me, 2)
    sib = sibling_of(me)
    width = outs[0].shape[1]
    half_tiles = outs[0].shape[0] // TILE // 2
    num = len(acts)
    total = num * 2 * half_tiles

    def tile_of(step):
        pos = step % (2 * half_tiles)
        if pos < half_tiles:
            return (1 - core) * half_tiles + pos
        return core * half_tiles + pos - half_tiles

    def cols(tile):
        return pl.ds(pl.multiple_of(tile * TILE, TILE), TILE)

    def load_lhs(step):
        return pltpu.make_async_copy(acts[step // (2 * half_tiles)].at[:, cols(tile_of(step))], lhs.at[step % 2], lhs_sem.at[step % 2])

    def load_rhs(which):
        return pltpu.make_async_copy(grads[which], rhs.at[which % 2], rhs_sem.at[which % 2])

    def part_copy(which, t):
        slot = which * half_tiles + t
        return remote(sbuf.at[t], rbuf.at[slot], ps.at[slot], pr.at[slot], sib)

    def out_rows(which, t):
        return outs[which].at[cols(core * half_tiles + t), :]

    def sum_copy(which, t):
        slot = which * half_tiles + t
        return remote(obuf.at[t % 2], out_rows(which, t), os_.at[slot], or_.at[slot], sib)

    def own_copy(which, t):
        return pltpu.make_async_copy(obuf.at[t % 2], out_rows(which, t), ol.at[which * half_tiles + t])

    load_rhs(0).start()
    load_lhs(0).start()
    greet([sib])
    small_copy = remote(small_ref, small_in, ss, sr, sib)
    small_copy.start()
    for step in range(total):
        which, pos = step // (2 * half_tiles), step % (2 * half_tiles)
        if step + 1 < total:
            load_lhs(step + 1).start()
        if pos == 0:
            load_rhs(which).wait()
            if which + 1 < num:
                load_rhs(which + 1).start()
        load_lhs(step).wait()
        left[...] = lhs[step % 2].T
        t = pos % half_tiles
        if pos < half_tiles:
            if which:
                part_copy(which - 1, t).wait_send()

            def part(i, carry):
                at = pl.ds(pl.multiple_of(i * CHUNK, CHUNK), CHUNK)
                sbuf[t, :, at] = mm(left[...], rhs[which % 2, :, at])
                return carry
            lax.fori_loop(0, width // CHUNK, part, 0)
            part_copy(which, t).start()
        else:
            before = which * half_tiles + t - 2
            if before >= 0:
                sum_copy(before // half_tiles, before % half_tiles).wait_send()
                own_copy(before // half_tiles, before % half_tiles).wait()
            part_copy(which, t).wait_recv()
            slot = which * half_tiles + t

            def whole(i, carry):
                at = pl.ds(pl.multiple_of(i * CHUNK, CHUNK), CHUNK)
                obuf[t % 2, :, at] = mm(left[...], rhs[which % 2, :, at]) + rbuf[slot, :, at]
                return carry
            lax.fori_loop(0, width // CHUNK, whole, 0)
            sum_copy(which, t).start()
            own_copy(which, t).start()
    small_copy.wait()
    small_out[...] = small_ref[...] + small_in[...]
    for t in range(half_tiles):
        part_copy(num - 1, t).wait_send()
        if t >= half_tiles - 2:
            sum_copy(num - 1, t).wait_send()
            own_copy(num - 1, t).wait()
    for which in range(num):
        for t in range(half_tiles):
            sum_copy(which, t).wait_recv()


def weight_grads(acts, grads, small):
    num = len(acts)
    rows = acts[0].shape[0]
    depth, width = acts[0].shape[1], grads[0].shape[1]
    half_tiles = depth // TILE // 2
    slots = num * half_tiles
    anyspec = pl.BlockSpec(memory_space=pl.ANY)
    vmem = pl.BlockSpec(memory_space=pltpu.VMEM)
    dma = pltpu.SemaphoreType.DMA

    def kern(*refs):
        weights_kernel(refs[:num], refs[num:2 * num], refs[2 * num], refs[2 * num + 1:3 * num + 1], *refs[3 * num + 1:])
    return pl.pallas_call(
        kern,
        out_shape=tuple(jax.ShapeDtypeStruct((depth, width), F32) for _ in range(num)) + (jax.ShapeDtypeStruct(small.shape, F32),),
        in_specs=[anyspec] * (2 * num) + [vmem],
        out_specs=tuple([anyspec] * num + [vmem]),
        scratch_shapes=[pltpu.VMEM((2, rows, TILE), BF), pltpu.VMEM((TILE, rows), BF), pltpu.VMEM((2, rows, width), BF),
                        pltpu.VMEM((half_tiles, TILE, width), F32), pltpu.VMEM((slots, TILE, width), F32), pltpu.VMEM((2, TILE, width), F32),
                        pltpu.VMEM(small.shape, F32), dma((2,)), dma((2,)), dma((slots,)), dma((slots,)), dma((slots,)), dma((slots,)), dma((slots,)), dma, dma],
        compiler_params=pltpu.CompilerParams(collective_id=2, has_side_effects=True, vmem_limit_bytes=63 << 20),
        cost_estimate=cost(num), name='weight_grads',
    )(*acts, *grads, small)


def solution(mesh):
    num_devs = mesh.shape[BATCH_AXIS]

    def local_step(feat_a, feat_b, w_one, w_two, w_three, g_one, b_one, g_two, b_two, lam_off):
        first = (lax.axis_index(BATCH_AXIS) % 2) == 0
        feat = gather_rows(jnp.stack([feat_a, feat_b]), num_devs)
        g_one, b_one, g_two, b_two = (v.reshape(1, -1) for v in (g_one, b_one, g_two, b_two))
        act_one, norm_one, inv_one = layer(feat, w_one, g_one, b_one)
        act_two, norm_two, inv_two = layer(act_one, w_two, g_two, b_two)
        emb, norm_out, inv_out, other = embed(act_two, w_three)
        grad_proj, loss = corr_back(lam_off, emb, other, norm_out, inv_out)
        loss_val = jnp.where(first, jnp.sum(loss), 0.0)
        grad_two, dg_two, db_two = layer_back(grad_proj, w_three, norm_two, inv_two, g_two, b_two)
        grad_one, dg_one, db_one = layer_back(grad_two, w_two, norm_one, inv_one, g_one, b_one)
        zero = jnp.zeros_like(dg_one)
        small = jnp.concatenate([dg_one, db_one, dg_two, db_two, zero + loss_val, zero, zero, zero])
        dw_three, dw_two, dw_one, small = weight_grads((act_two, act_one, feat), (grad_proj, grad_two, grad_one), small)
        return (small[4, 0], dw_one, dw_two, dw_three, small[0], small[1], small[2], small[3])

    row_spec = P(BATCH_AXIS, None)
    return jax.shard_map(local_step, mesh=mesh, in_specs=(row_spec, row_spec, P(), P(), P(), P(), P(), P(), P(), P()), out_specs=(P(), P(), P(), P(), P(), P(), P(), P()), check_vma=False)
```

time: 1460 us -> 407 us (0.28)
  waiting for transfers between devices: 1070 us -> 0 us
  Pallas kernels: 0 us -> 364 us
  blocking collectives: 202 us -> 0 us
  matrix products: 77.8 us -> 0 us
  local copies, waits for them, and re-layouts: 71.2 us -> 37.9 us
  other arithmetic: 19.1 us -> 2.48 us
  between operations: 17.8 us -> 2.03 us
    psum x3 -> x0, waiting for transfers between devices: 1070 us -> none  [the longest x1 672 us: local_step(): lax.psum((dw_one, dw_two, dw_three, dg_one, db_one, dg_two, db_two), BATC...]
    pallas_call x0 -> x8, Pallas kernels: none -> 364 us  [the longest x1 87.5 us: weight_grads(): pl.pallas_call(kern, out_shape=tuple((jax.ShapeDtypeStruct((depth, width)...]
    psum x5 -> x0, blocking collectives: 202 us -> none  [the longest x3 122 us: global_norm(): lax.psum(jnp.stack([jnp.sum(pre, axis=1), jnp.sum(pre * pre, axis=1)]), B...]
    dot_general x11 -> x0, matrix products: 77.8 us -> none  [the longest x1 10 us: local_step(): jnp.einsum('ne,de->nd', emb[1], grad_c, preferred_element_type=jnp.float32)]
    gather x1 -> x0, local copies, waits for them, and re-layouts: 33.2 us -> none  [corr_loss(): diag_c = jnp.diagonal(corr)]
    unnamed x47 -> x19, local copies, waits for them, and re-layouts: 38 us -> 33.7 us
  transfers between devices with their start and end apart: 3 -> 0, of which waited for: 3 -> 0; matrix products, arithmetic and copies ran while one was open for 4% -> 0% of each run, Pallas kernels for 0% -> 0%
where the time goes in v1:
time: 407 us; the launch traced here: 406 us
  Pallas kernels  364 us (89%)
  local copies, waits for them, and re-layouts  37.9 us (9%)
    pallas_call x1, Pallas kernels, weight_grads(): pl.pallas_call(kern, out_shape=tuple((jax.ShapeDtypeStruct((depth, width)...  87.5 us
    pallas_call x1, Pallas kernels, gather_rows(): pl.pallas_call(functools.partial(gather_kernel, rows), out_shape=jax.Shap...  82 us
    pallas_call x2, Pallas kernels, layer_back(): pl.pallas_call(back_kernel, grid=(width // TILE,), out_shape=(jax.ShapeDt...  60.7 us
    pallas_call x2, Pallas kernels, layer(): pl.pallas_call(layer_kernel, grid=(width // TILE,), out_shape=(jax.ShapeD...  57.3 us
    pallas_call x1, Pallas kernels, corr_back(): pl.pallas_call(corr_kernel, grid=(width // TILE,), out_shape=(jax.ShapeDt...  46.1 us
    unnamed x19, local copies, waits for them, and re-layouts  33.7 us
    pallas_call x1, Pallas kernels, embed(): pl.pallas_call(embed_kernel, grid=(tiles,), out_shape=(jax.ShapeDtypeStru...  30.3 us

profile of v1, /device:TPU:0, one launch (start us, length us, event | category | flops | bytes accessed | tf_op | source)
XLA Modules:
  0.0 406.2 jit_solution(16423200996984368168)
XLA Ops:
  1.3 1.9 pad_maximum_fusion.own_ref
  3.2 82.0 %gather_rows.1.x_ref.refs_2_ = bf16[2048,2048]{1,0:T(8,128)(2,1)} custom-call(bf16[2,64,2048]{2,1,0:T(8,128)(2,1)} %pad_maximum_fusion.own_ref), custom_call_target="tpu_custom_call" | custom-call | tf_op jit(solution)/shard_map/gather_rows/pallas_call | solution.py:157
  85.2 28.6 %layer.2 = (bf16[2048,2048]{1,0:T(8,128)(2,1)}, f32[2048,2048]{1,0:T(8,128)}, f32[1,2048]{1,0:T(1,128)}) custom-call(bf16[2048,2048]{1,0:T(8,128)(2,1)} %gather_rows.1.x_ref.refs_2_, bf16[2048,2048]{1,0:T(8,128)(2,1)} %w_ref.5, f32[1,2048]{1,0:T(1,128)} %bitcast.25, f32[1,2048]{1,0:T(1,128)} %bitcast.27), custom_call_target="tpu_custom_call" | custom-call | flops 17179869184 | bytes 41943040 | tf_op jit(solution)/shard_map/layer/pallas_call | solution.py:221
  113.8 28.7 %layer.3 = (bf16[2048,2048]{1,0:T(8,128)(2,1)}, f32[2048,2048]{1,0:T(8,128)}, f32[1,2048]{1,0:T(1,128)}) custom-call(bf16[2048,2048]{1,0:T(8,128)(2,1)} %get-tuple-element.30.x_ref.refs_1_, bf16[2048,2048]{1,0:T(8,128)(2,1)} %w_ref.9, f32[1,2048]{1,0:T(1,128)} %bitcast.21, f32[1,2048]{1,0:T(1,128)} %bitcast.23), custom_call_target="tpu_custom_call" | custom-call | flops 17179869184 | bytes 41943040 | tf_op jit(solution)/shard_map/layer/pallas_call | solution.py:221
  142.5 30.3 %embed.1 = (bf16[2048,2048]{1,0:T(8,128)(2,1)}, f32[2048,2048]{1,0:T(8,128)}, f32[1,2048]{1,0:T(1,128)}, bf16[2048,2048]{1,0:T(8,128)(2,1)}) custom-call(bf16[2048,2048]{1,0:T(8,128)(2,1)} %get-tuple-element.31.x_ref.refs_0_, bf16[2048,2048]{1,0:T(8,128)(2,1)} %w_ref.8), custom_call_target="tpu_custom_call" | custom-call | flops 17179869184 | bytes 41943040 | tf_op jit(solution)/shard_map/embed/pallas_call | solution.py:268
  172.8 46.1 %corr_back.1 = (bf16[2048,2048]{1,0:T(8,128)(2,1)}, f32[8,512]{1,0:T(8,128)}) custom-call(f32[1]{0:T(128)} %bitcast.12.lam_ref, bf16[2048,2048]{1,0:T(8,128)(2,1)} %get-tuple-element.32.emb_ref, bf16[2048,2048]{1,0:T(8,128)(2,1)} %get-tuple-element.33.other_ref, f32[2048,2048]{1,0:T(8,128)} %get-tuple-element.34.norm_ref, f32[1,2048]{1,0:T(1,128)} %get-tuple-element.35.inv_ref), custom_call_target="tpu_custom_call" | custom-call | flops 34359738368 | bytes 41943040 | tf_op jit(solution)/shard_map/corr_back/pallas_call | solution.py:322
  218.8 30.3 %layer_back.2 = (bf16[2048,2048]{1,0:T(8,128)(2,1)}, f32[1,2048]{1,0:T(1,128)}, f32[1,2048]{1,0:T(1,128)}) custom-call(bf16[2048,2048]{1,0:T(8,128)(2,1)} %get-tuple-element.36.d_ref.refs_3_, bf16[2048,2048]{1,0:T(8,128)(2,1)} %w_ref.8, f32[2048,2048]{1,0:T(8,128)} %get-tuple-element.37.norm_ref, f32[1,2048]{1,0:T(1,128)} %get-tuple-element.38.inv_ref, ...), custom_call_target="tpu_custom_call" | custom-call | flops 17179869184 | bytes 41943040 | tf_op jit(solution)/shard_map/layer_back/pallas_call | solution.py:362
  249.1 0.6 reduce_sum.9
  250.4 0.0 copy-start.2
  250.4 0.0 copy-start.3
  250.4 30.4 %layer_back.3 = (bf16[2048,2048]{1,0:T(8,128)(2,1)}, f32[1,2048]{1,0:T(1,128)}, f32[1,2048]{1,0:T(1,128)}) custom-call(bf16[2048,2048]{1,0:T(8,128)(2,1)} %get-tuple-element.39.d_ref.refs_4_, bf16[2048,2048]{1,0:T(8,128)(2,1)} %w_ref.9, f32[2048,2048]{1,0:T(8,128)} %get-tuple-element.40.norm_ref, f32[1,2048]{1,0:T(1,128)} %get-tuple-element.41.inv_ref, ...), custom_call_target="tpu_custom_call" | custom-call | flops 17179869184 | bytes 41943040 | tf_op jit(solution)/shard_map/layer_back/pallas_call | solution.py:362
  280.8 0.0 copy-done.2
  280.8 0.0 copy-done.3
  280.8 1.4 concatenate.7.refs_6_
  282.3 87.5 %weight_grads.1 = (f32[2048,2048]{1,0:T(8,128)}, f32[2048,2048]{1,0:T(8,128)}, f32[2048,2048]{1,0:T(8,128)}, f32[8,2048]{1,0:T(8,128)}) custom-call(bf16[2048,2048]{1,0:T(8,128)(2,1)} %get-tuple-element.31.x_ref.refs_0_, bf16[2048,2048]{1,0:T(8,128)(2,1)} %get-tuple-element.30.x_ref.refs_1_, bf16[2048,2048]{1,0:T(8,128)(2,1)} %gather_rows.1.x_ref.refs_2_, ...), custom_call_target="tpu_custom_call" | custom-call | flops 51539607552 | bytes 41943040 | tf_op jit(solution)/shard_map/weight_grads/pallas_call | solution.py:475
  369.8 1.2 slice.15
  371.0 1.6 fusion
  372.6 13.5 %copy.22 = f32[2048,2048]{1,0:T(8,128)} copy(f32[2048,2048]{1,0:T(8,128)} %get-tuple-element.65) | data formatting | bytes 33554432
  386.1 2.9 copy-done
  389.0 8.5 %copy.23 = f32[2048,2048]{1,0:T(8,128)} copy(f32[2048,2048]{1,0:T(8,128)S(1)} %copy-done) | data formatting | bytes 33554432
  397.5 0.0 slice-done
  397.5 1.4 slice-done.2
  398.9 1.2 slice-done.3
  400.1 6.2 %copy.24 = f32[2048,2048]{1,0:T(8,128)} copy(f32[2048,2048]{1,0:T(8,128)S(1)} %bitcast.14) | data formatting | bytes 33554432
  (11 shorter events, 0.0 us)
Async XLA Ops:
  218.8 30.3 %copy-start.1 = (f32[8,512]{1,0:T(8,128)S(1)}, f32[8,512]{1,0:T(8,128)}, u32[]{:S(2)}) copy-start(f32[8,512]{1,0:T(8,128)} %get-tuple-element.47) | copy-start | bytes 49156
  250.4 30.4 %copy-start.2 = (f32[1,2048]{1,0:T(1,128)S(1)}, f32[1,2048]{1,0:T(1,128)}, u32[]{:S(2)}) copy-start(f32[1,2048]{1,0:T(1,128)} %get-tuple-element.45) | copy-start | bytes 24580
  250.4 30.4 %copy-start.3 = (f32[1,2048]{1,0:T(1,128)S(1)}, f32[1,2048]{1,0:T(1,128)}, u32[]{:S(2)}) copy-start(f32[1,2048]{1,0:T(1,128)} %get-tuple-element.46) | copy-start | bytes 24580
  372.6 16.4 %copy-start = (f32[2048,2048]{1,0:T(8,128)S(1)}, f32[2048,2048]{1,0:T(8,128)}, u32[]{:S(2)}) copy-start(f32[2048,2048]{1,0:T(8,128)} %get-tuple-element.66) | copy-start | bytes 50331652
  372.6 24.9 %slice-start = ((s8[16777216]{0:T(1024)(128)(4,1)}), s8[4194304]{0:T(1024)(128)(4,1)S(1)}, s32[]{:S(2)}) async-start(s8[16777216]{0:T(1024)(128)(4,1)} %bitcast.13), calls=%async_computation | async-start | bytes 8388608
  372.6 24.9 %slice-start.1 = ((s8[16777216]{0:T(1024)(128)(4,1)}), s8[4194304]{0:T(1024)(128)(4,1)S(1)}, s32[]{:S(2)}) async-start(s8[16777216]{0:T(1024)(128)(4,1)} %bitcast.13), calls=%async_computation.1 | async-start | bytes 8388608
  389.0 9.9 %slice-start.2 = ((s8[16777216]{0:T(1024)(128)(4,1)}), s8[4194304]{0:T(1024)(128)(4,1)S(1)}, s32[]{:S(2)}) async-start(s8[16777216]{0:T(1024)(128)(4,1)} %bitcast.13), calls=%async_computation.2 | async-start | bytes 8388608
  389.0 11.1 %slice-start.3 = ((s8[16777216]{0:T(1024)(128)(4,1)}), s8[4194304]{0:T(1024)(128)(4,1)S(1)}, s32[]{:S(2)}) async-start(s8[16777216]{0:T(1024)(128)(4,1)} %bitcast.13), calls=%async_computation.3 | async-start | bytes 8388608

commit v2 on v0

v2 whole, which is shorter than its diff:
```python
import functools

import jax
import jax.numpy as jnp
from jax import lax
from jax.experimental import pallas as pl
from jax.experimental.pallas import tpu as pltpu
from jax.sharding import PartitionSpec as P

NORM_EPS = 1e-5
BATCH_AXIS = 'data'
MESH_ID = pl.DeviceIdType.MESH
TILE = 256
CHUNK = 512
BF = jnp.bfloat16
F32 = jnp.float32


def mm(lhs, rhs, lhs_dim=1, rhs_dim=0):
    return lax.dot_general(lhs, rhs, (((lhs_dim,), (rhs_dim,)), ((), ())), preferred_element_type=F32)


def fold(val):
    return jnp.sum(val.reshape(val.shape[0] // 8, 8, val.shape[1]), axis=0)


def sibling_of(me):
    return me + 1 - 2 * lax.rem(me, 2)


def greet(peers):
    barrier = pltpu.get_barrier_semaphore()
    for peer in peers:
        pl.semaphore_signal(barrier, inc=1, device_id=(peer,), device_id_type=MESH_ID)
    pl.semaphore_wait(barrier, len(peers))


def remote(src, dst, send_sem, recv_sem, dev):
    return pltpu.make_async_remote_copy(src_ref=src, dst_ref=dst, send_sem=send_sem, recv_sem=recv_sem, device_id=(dev,), device_id_type=MESH_ID)


def gather_kernel(rows, feat_a, feat_b, w_hbm, g_ref, b_ref, out_ref, act_out, pre_out, mean_ref, inv_ref, buf, w_ref, pre, act, tot, sqr,
                  own_sem, sib_s, sib_r, send_sem, recv_sem, w_sem, out_sem, pre_sem, act_sem):
    load_w = pltpu.make_async_copy(w_hbm, w_ref, w_sem)
    load_w.start()
    me = lax.axis_index(BATCH_AXIS)
    core = lax.rem(me, 2)
    sib = sibling_of(me)
    chip = me // 2
    xpos = lax.rem(chip, 2)
    ypos = lax.rem(chip // 2, 2)
    zpos = chip // 4
    x_dev = me + 2 - 4 * xpos
    y_dev = me + 4 - 8 * ypos
    up_dev = jnp.minimum(zpos + 1, 3) * 8 + lax.rem(me, 8)
    down_dev = jnp.maximum(zpos - 1, 0) * 8 + lax.rem(me, 8)
    barrier = pltpu.get_barrier_semaphore()
    for peer in (sib, x_dev, y_dev):
        pl.semaphore_signal(barrier, inc=1, device_id=(peer,), device_id_type=MESH_ID)
    has_up = zpos < 3
    has_down = zpos > 0

    @pl.when(has_up)
    def _():
        pl.semaphore_signal(barrier, inc=1, device_id=(up_dev,), device_id_type=MESH_ID)

    @pl.when(has_down)
    def _():
        pl.semaphore_signal(barrier, inc=1, device_id=(down_dev,), device_id_type=MESH_ID)
    pl.semaphore_wait(barrier, 3 + (1 - (zpos + 1) // 4) + (zpos + 3) // 4)

    def half(idx, part):
        return buf.at[pl.ds(pl.multiple_of(idx * 2 * rows + part * rows, rows), rows), :]

    for which, mine, theirs in ((0, feat_a, feat_b), (1, feat_b, feat_a)):
        @pl.when(core == which)
        def _(mine=mine, theirs=theirs):
            own = pltpu.make_async_copy(mine, half(chip, core), own_sem)
            own.start()
            to_sib = remote(theirs, half(chip, core), sib_s, sib_r, sib)
            to_sib.start()
            own.wait()
            to_sib.wait()

    def piece(idx, part, way, dev):
        return remote(half(idx, part), half(idx, part), send_sem.at[idx * 2 + part, way], recv_sem.at[idx, part], dev)

    def blk(xx, yy, zz):
        return (zz * 2 + yy) * 2 + xx

    def column(zz, part, going_up, going_down):
        idx = blk(xpos, ypos, zz)
        piece(idx, part, 0, x_dev).start()
        piece(idx, part, 1, y_dev).start()
        if going_up:
            @pl.when(has_up)
            def _():
                piece(idx, part, 2, up_dev).start()
        if going_down:
            @pl.when(has_down)
            def _():
                piece(idx, part, 3, down_dev).start()

    def arrived(idx, part):
        piece(idx, part, 0, x_dev).wait_recv()

    def across(zz):
        idx_x = blk(1 - xpos, ypos, zz)
        arrived(idx_x, 0)
        piece(idx_x, 0, 1, y_dev).start()
        idx_y = blk(xpos, 1 - ypos, zz)
        arrived(idx_y, 1)
        piece(idx_y, 1, 0, x_dev).start()

    def plane_rows(zz):
        return pl.ds(pl.multiple_of(zz * 8 * rows, 8 * rows), 8 * rows)

    def feat_copy(zz):
        return pltpu.make_async_copy(buf.at[plane_rows(zz), :], out_ref.at[plane_rows(zz), :], out_sem.at[zz])

    def pre_copy(zz):
        return pltpu.make_async_copy(pre.at[plane_rows(zz), :], pre_out.at[plane_rows(zz), :], pre_sem.at[zz])

    def multiply(zz):
        arrived(blk(1 - xpos, ypos, zz), 1)
        arrived(blk(xpos, 1 - ypos, zz), 0)
        arrived(blk(1 - xpos, 1 - ypos, zz), 0)
        arrived(blk(1 - xpos, 1 - ypos, zz), 1)
        feat_copy(zz).start()

        def step(i, carry):
            at = pl.ds(pl.multiple_of(i * CHUNK, CHUNK), CHUNK)
            val = mm(buf[plane_rows(zz), :], w_ref[:, at])
            pre[plane_rows(zz), at] = val
            tot[:, at] += fold(val)
            sqr[:, at] += fold(val * val)
            return carry
        lax.fori_loop(0, pre.shape[1] // CHUNK, step, 0)
        pre_copy(zz).start()

    for part in range(2):
        column(zpos, part, True, True)
    tot[...] = jnp.zeros_like(tot)
    sqr[...] = jnp.zeros_like(sqr)
    load_w.wait()

    def level(dist, carry):
        for sign in (-1, 1):
            zz = zpos + sign * dist

            @pl.when(jnp.logical_and(zz >= 0, zz < 4))
            def _(zz=zz, sign=sign):
                for part in range(2):
                    arrived(blk(xpos, ypos, zz), part)
                    column(zz, part, sign < 0, sign > 0)
            near = zpos + sign * (dist - 1)

            @pl.when(jnp.logical_and(jnp.logical_and(near >= 0, near < 4), dist > (1 if sign > 0 else 0)))
            def _(near=near):
                across(near)
            done = zpos + sign * (dist - 2)

            @pl.when(jnp.logical_and(jnp.logical_and(done >= 0, done < 4), dist > (2 if sign > 0 else 1)))
            def _(done=done):
                multiply(done)
        return carry
    lax.fori_loop(1, 6, level, 0)
    count = buf.shape[0]
    mean = jnp.sum(tot[...], axis=0, keepdims=True) / count
    inv = lax.rsqrt(jnp.sum(sqr[...], axis=0, keepdims=True) / count - mean * mean + NORM_EPS)
    mean_ref[...] = mean
    inv_ref[...] = inv

    def act_copy(i):
        at = pl.ds(pl.multiple_of(i * TILE, TILE), TILE)
        return pltpu.make_async_copy(act.at[at, :], act_out.at[at, :], act_sem.at[i])

    def fin(i, carry):
        def part(k, carry):
            at = pl.ds(pl.multiple_of(i * TILE + k * 32, 32), 32)
            norm = (pre[at, :] - mean_ref[...]) * inv_ref[...]
            act[at, :] = jnp.maximum(norm * g_ref[...] + b_ref[...], 0.0).astype(BF)
            return carry
        lax.fori_loop(0, TILE // 32, part, 0)
        act_copy(i).start()
        return carry
    lax.fori_loop(0, count // TILE, fin, 0)

    def drain(zz, carry):
        col = blk(xpos, ypos, zz)
        for part in range(2):
            piece(col, part, 0, x_dev).wait_send()
            piece(col, part, 1, y_dev).wait_send()

            @pl.when(jnp.logical_and(has_up, zz <= zpos))
            def _(part=part):
                piece(col, part, 2, up_dev).wait_send()

            @pl.when(jnp.logical_and(has_down, zz >= zpos))
            def _(part=part):
                piece(col, part, 3, down_dev).wait_send()
        piece(blk(1 - xpos, ypos, zz), 0, 1, y_dev).wait_send()
        piece(blk(xpos, 1 - ypos, zz), 1, 0, x_dev).wait_send()
        feat_copy(zz).wait()
        pre_copy(zz).wait()
        return carry
    lax.fori_loop(0, 4, drain, 0)

    def act_wait(i, carry):
        act_copy(i).wait()
        return carry
    lax.fori_loop(0, count // TILE, act_wait, 0)


def gather_layer(feat_a, feat_b, w, gain, bias, num_devs):
    rows, depth = feat_a.shape
    count, width = num_devs * rows, w.shape[1]
    chips = num_devs // 2
    dma = pltpu.SemaphoreType.DMA
    hbm, vmem = pl.BlockSpec(memory_space=pl.ANY), pl.BlockSpec(memory_space=pltpu.VMEM)
    vec = jax.ShapeDtypeStruct((1, width), F32)
    return pl.pallas_call(
        functools.partial(gather_kernel, rows),
        out_shape=(jax.ShapeDtypeStruct((count, depth), BF), jax.ShapeDtypeStruct((count, width), BF), jax.ShapeDtypeStruct((count, width), F32), vec, vec),
        in_specs=[vmem, vmem, hbm, vmem, vmem],
        out_specs=(hbm, hbm, hbm, vmem, vmem),
        scratch_shapes=[pltpu.VMEM((count, depth), BF), pltpu.VMEM(w.shape, BF), pltpu.VMEM((count, width), F32), pltpu.VMEM((count, width), BF),
                        pltpu.VMEM((8, width), F32), pltpu.VMEM((8, width), F32), dma, dma, dma,
                        dma((2 * chips, 4)), dma((chips, 2)), dma, dma((4,)), dma((4,)), dma((count // TILE,))],
        compiler_params=pltpu.CompilerParams(collective_id=0, has_side_effects=True, vmem_limit_bytes=60 << 20),
        name='gather_layer',
    )(feat_a, feat_b, w, gain, bias)


def at_chunk(i):
    return pl.ds(pl.multiple_of(i * CHUNK, CHUNK), CHUNK)


def at_tile(i):
    return pl.ds(pl.multiple_of(i * TILE, TILE), TILE)


def any_spec():
    return pl.BlockSpec(memory_space=pl.ANY)


def now(j, tiles):
    return jnp.minimum(j, tiles - 1)


def past(j):
    return jnp.maximum(j - 1, 0)


def col_now(rows, tiles):
    return pl.BlockSpec((rows, TILE), lambda j: (0, now(j, tiles)))


def col_past(rows):
    return pl.BlockSpec((rows, TILE), lambda j: (0, past(j)))


def row_now(cols, tiles):
    return pl.BlockSpec((TILE, cols), lambda j: (now(j, tiles), 0))


def row_past(cols):
    return pl.BlockSpec((TILE, cols), lambda j: (past(j), 0))


def row_same(cols):
    return pl.BlockSpec((TILE, cols), lambda j: (j, 0))


def col_same(rows):
    return pl.BlockSpec((rows, TILE), lambda j: (0, j))


def params(**kw):
    return pltpu.CompilerParams(dimension_semantics=('arbitrary',), vmem_limit_bytes=60 << 20, **kw)


def cost(units):
    return pl.CostEstimate(flops=int(units * 2 * 2048 ** 3), bytes_accessed=40 << 20, transcendentals=0)


def row_load(src, dst, sem, i):
    return pltpu.make_async_copy(src.at[at_chunk(i), :], dst.at[at_chunk(i), :], sem.at[i])


def col_load(src, dst, sem, i):
    return pltpu.make_async_copy(src.at[:, at_chunk(i)], dst.at[:, at_chunk(i)], sem.at[i])


def schedule(tiles, chunks, load, begin, mul, fin, end):
    j = pl.program_id(0)
    zero = (jnp.zeros((8, TILE), F32),) * 2

    @pl.when(j == 0)
    def _():
        for i in range(chunks):
            load(i).start()
        begin()

        def step(i, sums):
            load(i).wait()
            return mul(i, sums)
        end(lax.fori_loop(0, chunks, step, zero))

    @pl.when(jnp.logical_and(j > 0, j < tiles))
    def _():
        begin()
        sums = zero
        for i in range(chunks):
            fin(i)
            sums = mul(i, sums)
        end(sums)

    @pl.when(j == tiles)
    def _():
        def step(i, carry):
            fin(i)
            return carry
        lax.fori_loop(0, chunks, step, 0)


def row_sum(val):
    return jnp.sum(val, axis=0, keepdims=True)


def layer_kernel(tiles, x_hbm, w_ref, g_ref, b_ref, act_ref, norm_ref, inv_ref, x_ref, x_sem, pre, mean_s, inv_s):
    rows = x_ref.shape[0]

    def mul(i, sums):
        val = mm(x_ref[at_chunk(i), :], w_ref[...])
        pre[at_chunk(i), :] = val
        return sums[0] + fold(val), sums[1] + fold(val * val)

    def fin(i):
        norm = (pre[at_chunk(i), :] - mean_s[...]) * inv_s[...]
        norm_ref[at_chunk(i), :] = norm
        act_ref[at_chunk(i), :] = jnp.maximum(norm * g_ref[...] + b_ref[...], 0.0).astype(BF)

    def end(sums):
        mean = row_sum(sums[0]) / rows
        mean_s[...] = mean
        inv_s[...] = lax.rsqrt(row_sum(sums[1]) / rows - mean * mean + NORM_EPS)

    @pl.when(pl.program_id(0) > 0)
    def _():
        inv_ref[...] = inv_s[...]
    schedule(tiles, rows // CHUNK, functools.partial(row_load, x_hbm, x_ref, x_sem), lambda: None, mul, fin, end)


def layer(x, w, gain, bias):
    rows, width = x.shape[0], w.shape[1]
    tiles = width // TILE
    return pl.pallas_call(
        functools.partial(layer_kernel, tiles), grid=(tiles + 1,),
        out_shape=(jax.ShapeDtypeStruct((rows, width), BF), jax.ShapeDtypeStruct((rows, width), F32), jax.ShapeDtypeStruct((1, width), F32)),
        in_specs=[any_spec(), col_now(w.shape[0], tiles), col_past(1), col_past(1)],
        out_specs=(col_past(rows), col_past(rows), col_past(1)),
        scratch_shapes=[pltpu.VMEM(x.shape, BF), pltpu.SemaphoreType.DMA((rows // CHUNK,)), pltpu.VMEM((rows, TILE), F32), pltpu.VMEM((1, TILE), F32), pltpu.VMEM((1, TILE), F32)],
        compiler_params=params(), cost_estimate=cost(1), name='layer',
    )(x, w, gain, bias)


def share(hold, other_ref, send_sem, recv_sem, t):
    return remote(hold.at[t], other_ref.at[:, at_tile(t)], send_sem.at[t], recv_sem.at[t], sibling_of(lax.axis_index(BATCH_AXIS)))


def share_tiles(j, tiles, copy):
    @pl.when(j > 0)
    def _():
        copy(j - 1).start()

    @pl.when(j == tiles)
    def _():
        def last(t, carry):
            copy(t).wait()
            return carry
        lax.fori_loop(0, tiles, last, 0)


def embed_kernel(tiles, x_hbm, w_ref, emb_ref, norm_ref, inv_ref, other_ref, x_ref, x_sem, pre, mean_s, inv_s, hold, send_sem, recv_sem):
    rows = x_ref.shape[0]
    j = pl.program_id(0)

    @pl.when(j == 0)
    def _():
        greet([sibling_of(lax.axis_index(BATCH_AXIS))])

    def mul(i, sums):
        val = mm(x_ref[at_chunk(i), :], w_ref[...])
        pre[at_chunk(i), :] = val
        return sums[0] + fold(val), sums[1] + fold(val * val)

    def fin(i):
        norm = (pre[at_chunk(i), :] - mean_s[...]) * inv_s[...]
        norm_ref[at_chunk(i), :] = norm
        emb = norm.astype(BF)
        emb_ref[at_chunk(i), :] = emb
        hold[past(j), at_chunk(i), :] = emb

    def end(sums):
        mean = row_sum(sums[0]) / rows
        mean_s[...] = mean
        inv_s[...] = lax.rsqrt(row_sum(sums[1]) / rows - mean * mean + NORM_EPS)

    @pl.when(j > 0)
    def _():
        inv_ref[...] = inv_s[...]
    schedule(tiles, rows // CHUNK, functools.partial(row_load, x_hbm, x_ref, x_sem), lambda: None, mul, fin, end)
    share_tiles(j, tiles, functools.partial(share, hold, other_ref, send_sem, recv_sem))


def share_scratch(rows, tiles):
    return [pltpu.VMEM((tiles, rows, TILE), BF), pltpu.SemaphoreType.DMA((tiles,)), pltpu.SemaphoreType.DMA((tiles,))]


def embed(x, w):
    rows, width = x.shape[0], w.shape[1]
    tiles = width // TILE
    return pl.pallas_call(
        functools.partial(embed_kernel, tiles), grid=(tiles + 1,),
        out_shape=(jax.ShapeDtypeStruct((rows, width), BF), jax.ShapeDtypeStruct((rows, width), F32), jax.ShapeDtypeStruct((1, width), F32), jax.ShapeDtypeStruct((rows, width), BF)),
        in_specs=[any_spec(), col_now(w.shape[0], tiles)],
        out_specs=(col_past(rows), col_past(rows), col_past(1), any_spec()),
        scratch_shapes=[pltpu.VMEM(x.shape, BF), pltpu.SemaphoreType.DMA((rows // CHUNK,)), pltpu.VMEM((rows, TILE), F32), pltpu.VMEM((1, TILE), F32), pltpu.VMEM((1, TILE), F32)] + share_scratch(rows, tiles),
        compiler_params=params(collective_id=1, has_side_effects=True), cost_estimate=cost(1), name='embed',
    )(x, w)


def corr_kernel(lam_ref, emb_ref, other_ref, norm_ref, inv_ref, dout_ref, loss_ref, left, grad_c, scr):
    j = pl.program_id(0)
    rows, width = other_ref.shape
    scale = 1.0 / rows
    lam = lam_ref[0]

    @pl.when(j == 0)
    def _():
        loss_ref[...] = jnp.zeros_like(loss_ref)
    left[...] = emb_ref[...].T

    def corr_step(i, loss):
        at = pl.ds(pl.multiple_of(i * CHUNK, CHUNK), CHUNK)
        corr = mm(left[...], other_ref[:, at]) * scale
        row_id = lax.broadcasted_iota(jnp.int32, corr.shape, 0) + j * TILE
        col_id = lax.broadcasted_iota(jnp.int32, corr.shape, 1) + i * CHUNK
        on_diag = row_id == col_id
        miss = 1.0 - corr
        lam_corr = lam * corr
        grad_c[:, at] = jnp.where(on_diag, -2.0 * miss, 2.0 * lam_corr).astype(BF)
        return loss + fold(jnp.where(on_diag, miss * miss, lam_corr * corr))
    loss = lax.fori_loop(0, width // CHUNK, corr_step, jnp.zeros((8, CHUNK), F32), unroll=True)
    loss_ref[...] += loss

    def emb_step(i, carry):
        at = pl.ds(pl.multiple_of(i * CHUNK, CHUNK), CHUNK)
        val = mm(other_ref[at, :], grad_c[...], 1, 1) * scale
        scr[at, :] = val
        return carry[0] + fold(val), carry[1] + fold(val * norm_ref[at, :])
    zero = jnp.zeros((8, TILE), F32)
    tot, crs = lax.fori_loop(0, rows // CHUNK, emb_step, (zero, zero), unroll=True)
    mean_grad = jnp.sum(tot, axis=0, keepdims=True) / rows
    mean_cross = jnp.sum(crs, axis=0, keepdims=True) / rows
    inv = inv_ref[...]

    def fin(i, carry):
        at = pl.ds(pl.multiple_of(i * TILE, TILE), TILE)
        dout_ref[at, :] = (inv * (scr[at, :] - mean_grad - norm_ref[at, :] * mean_cross)).astype(BF)
        return carry
    lax.fori_loop(0, rows // TILE, fin, 0)


def corr_back(lam_off, emb, other, norm, inv):
    rows, width = emb.shape
    return pl.pallas_call(
        corr_kernel, grid=(width // TILE,),
        out_shape=(jax.ShapeDtypeStruct((rows, width), BF), jax.ShapeDtypeStruct((8, CHUNK), F32)),
        in_specs=[pl.BlockSpec(memory_space=pltpu.SMEM), col_same(rows), pl.BlockSpec(other.shape, lambda j: (0, 0), pipeline_mode=pl.Buffered(1)), col_same(rows), col_same(1)],
        out_specs=(col_same(rows), pl.BlockSpec((8, CHUNK), lambda j: (0, 0))),
        scratch_shapes=[pltpu.VMEM((TILE, rows), BF), pltpu.VMEM((TILE, width), BF), pltpu.VMEM((rows, TILE), F32)],
        compiler_params=params(), cost_estimate=cost(2), name='corr_back',
    )(lam_off.reshape(1), emb, other, norm, inv)


def back_kernel(tiles, layered, act_hbm, d_hbm, *refs):
    if layered:
        w_ref, pre_ref, mean_ref, scale_ref, inv_ref, g_ref, b_ref, g_old, dpre_ref, dg_ref, db_ref, dw_out = refs[:12]
        d_ref, d_sem, lhs, lhs_sem, sbuf, rbuf, ps, pr, os_, or_, ol, scr, norm_s, grad_s, cross_s = refs[12:]
    else:
        small_ref, dw_out, small_out = refs[:3]
        d_ref, d_sem, lhs, lhs_sem, sbuf, rbuf, ps, pr, os_, or_, ol, small_in, ss, sr = refs[3:]
    step = pl.program_id(0)
    rows, width = d_ref.shape
    half = sbuf.shape[0]
    chunks = width // CHUNK
    me = lax.axis_index(BATCH_AXIS)
    core = lax.rem(me, 2)
    sib = sibling_of(me)
    after = step - half
    if layered:
        turn, place = after // 3, lax.rem(after, 3)
        own_turn = jnp.logical_and(jnp.logical_and(after >= 0, after < 3 * half), place == 1)
        tile_turn = jnp.logical_and(jnp.logical_and(after >= 0, after < 3 * half), place != 1)
        last_step = 3 * half
    else:
        turn = after
        own_turn = after >= 0
        last_step = half - 1

    def load_left(q):
        mine = q // half
        tile = (mine * core + (1 - mine) * (1 - core)) * half + q - mine * half
        return pltpu.make_async_copy(act_hbm.at[:, at_tile(tile)], lhs.at[lax.rem(q, 2)], lhs_sem.at[lax.rem(q, 2)])

    def part_copy(t):
        return remote(sbuf.at[t], rbuf.at[t], ps.at[t], pr.at[t], sib)

    def result_rows(t):
        return dw_out.at[at_tile(core * half + t), :]

    def sum_copy(t):
        return remote(sbuf.at[t], result_rows(t), os_.at[t], or_.at[t], sib)

    def own_copy(t):
        return pltpu.make_async_copy(sbuf.at[t], result_rows(t), ol.at[t])

    def load_d(i):
        return col_load(d_hbm, d_ref, d_sem, i)

    def product(q, i):
        return mm(lhs[lax.rem(q, 2)], d_ref[:, at_chunk(i)], 0, 0)

    @pl.when(step == 0)
    def _():
        load_left(0).start()
        for i in range(chunks):
            load_d(i).start()
        load_left(1).start()
        greet([sib])
        if not layered:
            remote(small_ref, small_in, ss, sr, sib).start()
        load_left(0).wait()

        def first(i, carry):
            load_d(i).wait()
            sbuf[0, :, at_chunk(i)] = product(0, i)
            return carry
        lax.fori_loop(0, chunks, first, 0)
        part_copy(0).start()

    @pl.when(jnp.logical_and(step > 0, step < half))
    def _():
        load_left(step + 1).start()
        load_left(step).wait()
        for i in range(chunks):
            sbuf[step, :, at_chunk(i)] = product(step, i)
        part_copy(step).start()

    if layered:
        def mul(i, sums):
            val = mm(d_ref[at_chunk(i), :], w_ref[...], 1, 1)
            norm = (pre_ref[at_chunk(i), :] - mean_ref[...]) * scale_ref[...]
            val = jnp.where(norm * g_ref[...] + b_ref[...] > 0, val, 0.0)
            scr[at_chunk(i), :] = val
            norm_s[at_chunk(i), :] = norm
            return sums[0] + fold(val), sums[1] + fold(val * norm)

        def fin(i):
            dpre_ref[at_chunk(i), :] = (inv_ref[...] * (scr[at_chunk(i), :] * g_old[...] - grad_s[...] - norm_s[at_chunk(i), :] * cross_s[...])).astype(BF)
        zero = (jnp.zeros((8, TILE), F32),) * 2

        @pl.when(tile_turn)
        def _():
            sums = zero
            for i in range(rows // CHUNK):
                fin(i)
                sums = mul(i, sums)
            tot, crs = row_sum(sums[0]), row_sum(sums[1])
            db_ref[...] = tot
            dg_ref[...] = crs
            grad_s[...] = g_ref[...] * tot / rows
            cross_s[...] = g_ref[...] * crs / rows

        @pl.when(after == last_step)
        def _():
            def last(i, carry):
                fin(i)
                return carry
            lax.fori_loop(0, rows // CHUNK, last, 0)

    @pl.when(own_turn)
    def _():
        t = turn
        q = t + half

        @pl.when(t + 1 < half)
        def _():
            load_left(q + 1).start()
        load_left(q).wait()
        part_copy(t).wait()
        for i in range(chunks):
            sbuf[t, :, at_chunk(i)] = product(q, i) + rbuf[t, :, at_chunk(i)]
        sum_copy(t).start()
        own_copy(t).start()

    @pl.when(after == last_step)
    def _():
        def end(k, carry):
            sum_copy(k).wait()
            own_copy(k).wait()
            return carry
        lax.fori_loop(0, half, end, 0)
        if not layered:
            remote(small_ref, small_in, ss, sr, sib).wait()
            small_out[...] = small_ref[...] + small_in[...]


def layer_back(ident, act, grad, layer_args=None, small=None):
    rows, width = grad.shape
    depth = act.shape[1]
    half = depth // TILE // 2
    dma = pltpu.SemaphoreType.DMA
    hbm = any_spec()
    scratch = [pltpu.VMEM(grad.shape, BF), dma((width // CHUNK,)), pltpu.VMEM((2, rows, TILE), BF), dma((2,)), pltpu.VMEM((half, TILE, width), F32),
               pltpu.VMEM((half, TILE, width), F32)] + [dma((half,))] * 5
    dw = jax.ShapeDtypeStruct((depth, width), F32)
    if layer_args is not None:
        w, pre, mean, scale, inv, gain, bias = layer_args
        tiles = w.shape[0] // TILE

        def cur(s):
            return jnp.clip((2 * jnp.maximum(s - half, 0) + 1) // 3, 0, tiles - 1)

        def old(s):
            return jnp.clip((2 * jnp.maximum(s - half, 0) + 1) // 3 - 1, 0, tiles - 1)
        vec_cur = pl.BlockSpec((1, TILE), lambda s: (0, cur(s)))
        vec_old = pl.BlockSpec((1, TILE), lambda s: (0, old(s)))
        in_specs = [hbm, hbm, pl.BlockSpec((TILE, w.shape[1]), lambda s: (cur(s), 0)), pl.BlockSpec((rows, TILE), lambda s: (0, cur(s))),
                    vec_cur, vec_cur, vec_old, vec_cur, vec_cur, vec_old]
        out_specs = (pl.BlockSpec((rows, TILE), lambda s: (0, old(s))), vec_cur, vec_cur, hbm)
        vec = jax.ShapeDtypeStruct((1, depth), F32)
        out_shape = (jax.ShapeDtypeStruct((rows, depth), BF), vec, vec, dw)
        scratch += [pltpu.VMEM((rows, TILE), F32), pltpu.VMEM((rows, TILE), F32), pltpu.VMEM((1, TILE), F32), pltpu.VMEM((1, TILE), F32)]
        args = (act, grad, w, pre, mean, scale, inv, gain, bias, gain)
        steps = 2 * half + tiles + 1
    else:
        tiles = 0
        one = pl.BlockSpec(small.shape, lambda s: (0, 0))
        in_specs = [hbm, hbm, one]
        out_specs = (hbm, one)
        out_shape = (dw, jax.ShapeDtypeStruct(small.shape, F32))
        scratch += [pltpu.VMEM(small.shape, F32), dma, dma]
        args = (act, grad, small)
        steps = 2 * half
    return pl.pallas_call(
        functools.partial(back_kernel, tiles, layer_args is not None), grid=(steps,),
        out_shape=out_shape, in_specs=in_specs, out_specs=out_specs, scratch_shapes=scratch,
        compiler_params=params(collective_id=ident, has_side_effects=True), cost_estimate=cost(2), name='back_%d' % ident,
    )(*args)


def solution(mesh):
    num_devs = mesh.shape[BATCH_AXIS]

    def local_step(feat_a, feat_b, w_one, w_two, w_three, g_one, b_one, g_two, b_two, lam_off):
        first = lax.rem(lax.axis_index(BATCH_AXIS), 2) == 0
        g_one, b_one, g_two, b_two = (v.reshape(1, -1) for v in (g_one, b_one, g_two, b_two))
        feat, act_one, pre_one, mean_one, inv_one = gather_layer(feat_a, feat_b, w_one, g_one, b_one, num_devs)
        act_two, norm_two, inv_two = layer(act_one, w_two, g_two, b_two)
        emb, norm_out, inv_out, other = embed(act_two, w_three)
        grad_out, loss = corr_back(lam_off, emb, other, norm_out, inv_out)
        loss_val = jnp.where(first, jnp.sum(loss), 0.0)
        zero, one = jnp.zeros_like(g_two), jnp.ones_like(g_two)
        grad_two, dg_two, db_two, dw_three = layer_back(2, act_two, grad_out, (w_three, norm_two, zero, one, inv_two, g_two, b_two))
        grad_one, dg_one, db_one, dw_two = layer_back(3, act_one, grad_two, (w_two, pre_one, mean_one, inv_one, inv_one, g_one, b_one))
        small = jnp.concatenate([dg_one, db_one, dg_two, db_two, zero + loss_val, zero, zero, zero])
        dw_one, small = layer_back(4, feat, grad_one, small=small)
        return (small[4, 0], dw_one, dw_two, dw_three, small[0], small[1], small[2], small[3])

    row_spec = P(BATCH_AXIS, None)
    return jax.shard_map(local_step, mesh=mesh, in_specs=(row_spec, row_spec, P(), P(), P(), P(), P(), P(), P(), P()), out_specs=(P(), P(), P(), P(), P(), P(), P(), P()), check_vma=False)
```

time: 1460 us -> 374 us (0.26)
  waiting for transfers between devices: 1070 us -> 0 us
  Pallas kernels: 0 us -> 332 us
  blocking collectives: 202 us -> 0 us
  matrix products: 77.8 us -> 0 us
  local copies, waits for them, and re-layouts: 71.2 us -> 39.1 us
  other arithmetic: 19.1 us -> 0.6 us
  between operations: 17.8 us -> 2.05 us
    psum x3 -> x0, waiting for transfers between devices: 1070 us -> none  [the longest x1 672 us: local_step(): lax.psum((dw_one, dw_two, dw_three, dg_one, db_one, dg_two, db_two), BATC...]
    pallas_call x0 -> x7, Pallas kernels: none -> 332 us  [the longest x3 138 us: layer_back(): pl.pallas_call(functools.partial(back_kernel, tiles, layer_args is not No...]
    psum x5 -> x0, blocking collectives: 202 us -> none  [the longest x3 122 us: global_norm(): lax.psum(jnp.stack([jnp.sum(pre, axis=1), jnp.sum(pre * pre, axis=1)]), B...]
    dot_general x11 -> x0, matrix products: 77.8 us -> none  [the longest x1 10 us: local_step(): jnp.einsum('ne,de->nd', emb[1], grad_c, preferred_element_type=jnp.float32)]
    gather x1 -> x0, local copies, waits for them, and re-layouts: 33.2 us -> none  [corr_loss(): diag_c = jnp.diagonal(corr)]
    unnamed x47 -> x19, local copies, waits for them, and re-layouts: 38 us -> 33.7 us
  transfers between devices with their start and end apart: 3 -> 0, of which waited for: 3 -> 0; matrix products, arithmetic and copies ran while one was open for 4% -> 0% of each run, Pallas kernels for 0% -> 0%
where the time goes in v2:
time: 374 us; the launch traced here: 373 us
  Pallas kernels  332 us (89%)
  local copies, waits for them, and re-layouts  39.1 us (10%)
    pallas_call x3, Pallas kernels, layer_back(): pl.pallas_call(functools.partial(back_kernel, tiles, layer_args is not No...  138 us
    pallas_call x1, Pallas kernels, gather_layer(): pl.pallas_call(functools.partial(gather_kernel, rows), out_shape=(jax.Sha...  90.5 us
    pallas_call x1, Pallas kernels, corr_back(): pl.pallas_call(corr_kernel, grid=(width // TILE,), out_shape=(jax.ShapeDt...  46 us
    unnamed x19, local copies, waits for them, and re-layouts  33.7 us
    pallas_call x1, Pallas kernels, embed(): pl.pallas_call(functools.partial(embed_kernel, tiles), grid=(tiles + 1,),...  29.8 us
    pallas_call x1, Pallas kernels, layer(): pl.pallas_call(functools.partial(layer_kernel, tiles), grid=(tiles + 1,),...  27.3 us

profile of v2, /device:TPU:0, one launch (start us, length us, event | category | flops | bytes accessed | tf_op | source)
XLA Modules:
  0.0 373.5 jit_solution(12319114651570241580)
XLA Ops:
  0.6 90.5 %gather_layer.1 = (bf16[2048,2048]{1,0:T(8,128)(2,1)}, bf16[2048,2048]{1,0:T(8,128)(2,1)}, f32[2048,2048]{1,0:T(8,128)}, f32[1,2048]{1,0:T(1,128)}, f32[1,2048]{1,0:T(1,128)}) custom-call(bf16[64,2048]{1,0:T(8,128)(2,1)} %feat_a.1, bf16[64,2048]{1,0:T(8,128)(2,1)} %feat_b.1, bf16[2048,2048]{1,0:T(8,128)(2,1)} %w_hbm.1, f32[1,2048]{1,0:T(1,128)} %bitcast.17, ...), custom_call_target="tpu_custom_call" | custom-call | tf_op jit(solution)/shard_map/gather_layer/pallas_call | solution.py:222
  91.1 27.3 %layer.1 = (bf16[2048,2048]{1,0:T(8,128)(2,1)}, f32[2048,2048]{1,0:T(8,128)}, f32[1,2048]{1,0:T(1,128)}) custom-call(bf16[2048,2048]{1,0:T(8,128)(2,1)} %get-tuple-element.33.x_hbm.act_hbm, bf16[2048,2048]{1,0:T(8,128)(2,1)} %refs_0_.3, f32[1,2048]{1,0:T(1,128)} %bitcast.22, f32[1,2048]{1,0:T(1,128)} %bitcast.25), custom_call_target="tpu_custom_call" | custom-call | flops 17179869184 | bytes 41943040 | tf_op jit(solution)/shard_map/layer/pallas_call | solution.py:358
  118.4 29.8 %embed.1 = (bf16[2048,2048]{1,0:T(8,128)(2,1)}, f32[2048,2048]{1,0:T(8,128)}, f32[1,2048]{1,0:T(1,128)}, bf16[2048,2048]{1,0:T(8,128)(2,1)}) custom-call(bf16[2048,2048]{1,0:T(8,128)(2,1)} %get-tuple-element.34.x_hbm.act_hbm, bf16[2048,2048]{1,0:T(8,128)(2,1)} %refs_0_.2), custom_call_target="tpu_custom_call" | custom-call | flops 17179869184 | bytes 41943040 | tf_op jit(solution)/shard_map/embed/pallas_call | solution.py:424
  148.9 46.0 %corr_back.1 = (bf16[2048,2048]{1,0:T(8,128)(2,1)}, f32[8,512]{1,0:T(8,128)}) custom-call(f32[1]{0:T(128)} %bitcast.10.lam_ref, bf16[2048,2048]{1,0:T(8,128)(2,1)} %get-tuple-element.35.emb_ref, bf16[2048,2048]{1,0:T(8,128)(2,1)} %get-tuple-element.36.other_ref, f32[2048,2048]{1,0:T(8,128)} %get-tuple-element.37.norm_ref, f32[1,2048]{1,0:T(1,128)} %get-tuple-element.38.inv_ref), custom_call_target="tpu_custom_call" | custom-call | flops 34359738368 | bytes 41943040 | tf_op jit(solution)/shard_map/corr_back/pallas_call | solution.py:478
  194.9 0.6 broadcast_in_dim.6.refs_2_
  195.5 0.6 broadcast_in_dim.7.refs_3_
  196.1 52.9 %back_2.1 = (bf16[2048,2048]{1,0:T(8,128)(2,1)}, f32[1,2048]{1,0:T(1,128)}, f32[1,2048]{1,0:T(1,128)}, f32[2048,2048]{1,0:T(8,128)}) custom-call(bf16[2048,2048]{1,0:T(8,128)(2,1)} %get-tuple-element.34.x_hbm.act_hbm, bf16[2048,2048]{1,0:T(8,128)(2,1)} %get-tuple-element.39.d_hbm, bf16[2048,2048]{1,0:T(8,128)(2,1)} %refs_0_.2, ...), custom_call_target="tpu_custom_call" | custom-call | flops 34359738368 | bytes 41943040 | tf_op jit(solution)/shard_map/back_2/pallas_call | solution.py:658
  249.0 0.0 copy-start.1
  249.1 53.2 %back_3.1 = (bf16[2048,2048]{1,0:T(8,128)(2,1)}, f32[1,2048]{1,0:T(1,128)}, f32[1,2048]{1,0:T(1,128)}, f32[2048,2048]{1,0:T(8,128)}) custom-call(bf16[2048,2048]{1,0:T(8,128)(2,1)} %get-tuple-element.33.x_hbm.act_hbm, bf16[2048,2048]{1,0:T(8,128)(2,1)} %get-tuple-element.42.d_hbm, bf16[2048,2048]{1,0:T(8,128)(2,1)} %refs_0_.3, ...), custom_call_target="tpu_custom_call" | custom-call | flops 34359738368 | bytes 41943040 | tf_op jit(solution)/shard_map/back_3/pallas_call | solution.py:658
  302.2 0.0 copy-done.1
  302.2 0.6 reduce_sum.9
  303.5 0.0 copy-done.2
  303.5 0.0 copy-done.3
  303.5 1.4 concatenate.7.refs_0_
  305.0 32.0 %back_4.1 = (f32[2048,2048]{1,0:T(8,128)}, f32[8,2048]{1,0:T(8,128)}) custom-call(bf16[2048,2048]{1,0:T(8,128)(2,1)} %get-tuple-element.32.act_hbm, bf16[2048,2048]{1,0:T(8,128)(2,1)} %get-tuple-element.46.d_hbm, f32[8,2048]{1,0:T(8,128)} %concatenate.7.refs_0_), custom_call_target="tpu_custom_call" | custom-call | flops 34359738368 | bytes 41943040 | tf_op jit(solution)/shard_map/back_4/pallas_call | solution.py:658
  337.0 1.6 fusion
  338.6 1.2 slice.15
  339.8 13.5 %copy.22 = f32[2048,2048]{1,0:T(8,128)} copy(f32[2048,2048]{1,0:T(8,128)} %get-tuple-element.69) | data formatting | bytes 33554432
  353.3 2.9 copy-done
  356.2 8.5 %copy.23 = f32[2048,2048]{1,0:T(8,128)} copy(f32[2048,2048]{1,0:T(8,128)S(1)} %copy-done) | data formatting | bytes 33554432
  364.7 0.0 slice-done.1
  364.7 1.4 slice-done.2
  366.1 1.2 slice-done.3
  367.3 6.2 %copy.24 = f32[2048,2048]{1,0:T(8,128)} copy(f32[2048,2048]{1,0:T(8,128)S(1)} %bitcast.12) | data formatting | bytes 33554432
  (11 shorter events, 0.0 us)
Async XLA Ops:
  249.0 53.2 %copy-start.1 = (f32[8,512]{1,0:T(8,128)S(1)}, f32[8,512]{1,0:T(8,128)}, u32[]{:S(2)}) copy-start(f32[8,512]{1,0:T(8,128)} %get-tuple-element.51) | copy-start | bytes 49156
  249.0 54.5 %copy-start.2 = (f32[1,2048]{1,0:T(1,128)S(1)}, f32[1,2048]{1,0:T(1,128)}, u32[]{:S(2)}) copy-start(f32[1,2048]{1,0:T(1,128)} %get-tuple-element.49) | copy-start | bytes 24580
  249.1 54.5 %copy-start.3 = (f32[1,2048]{1,0:T(1,128)S(1)}, f32[1,2048]{1,0:T(1,128)}, u32[]{:S(2)}) copy-start(f32[1,2048]{1,0:T(1,128)} %get-tuple-element.50) | copy-start | bytes 24580
  339.8 16.4 %copy-start = (f32[2048,2048]{1,0:T(8,128)S(1)}, f32[2048,2048]{1,0:T(8,128)}, u32[]{:S(2)}) copy-start(f32[2048,2048]{1,0:T(8,128)} %get-tuple-element.70) | copy-start | bytes 50331652
  339.8 24.9 %slice-start = ((s8[16777216]{0:T(1024)(128)(4,1)}), s8[4194304]{0:T(1024)(128)(4,1)S(1)}, s32[]{:S(2)}) async-start(s8[16777216]{0:T(1024)(128)(4,1)} %bitcast.11), calls=%async_computation | async-start | bytes 8388608
  339.8 24.9 %slice-start.1 = ((s8[16777216]{0:T(1024)(128)(4,1)}), s8[4194304]{0:T(1024)(128)(4,1)S(1)}, s32[]{:S(2)}) async-start(s8[16777216]{0:T(1024)(128)(4,1)} %bitcast.11), calls=%async_computation.1 | async-start | bytes 8388608
  356.2 9.9 %slice-start.2 = ((s8[16777216]{0:T(1024)(128)(4,1)}), s8[4194304]{0:T(1024)(128)(4,1)S(1)}, s32[]{:S(2)}) async-start(s8[16777216]{0:T(1024)(128)(4,1)} %bitcast.11), calls=%async_computation.2 | async-start | bytes 8388608
  356.2 11.1 %slice-start.3 = ((s8[16777216]{0:T(1024)(128)(4,1)}), s8[4194304]{0:T(1024)(128)(4,1)S(1)}, s32[]{:S(2)}) async-start(s8[16777216]{0:T(1024)(128)(4,1)} %bitcast.11), calls=%async_computation.3 | async-start | bytes 8388608

commit v3 on v2

--- a/solution.py
+++ b/solution.py
@@ -77,10 +77,8 @@
         def _(mine=mine, theirs=theirs):
             own = pltpu.make_async_copy(mine, half(chip, core), own_sem)
             own.start()
-            to_sib = remote(theirs, half(chip, core), sib_s, sib_r, sib)
-            to_sib.start()
+            remote(theirs, half(chip, core), sib_s, sib_r, sib).start()
             own.wait()
-            to_sib.wait()
 
     def piece(idx, part, way, dev):
         return remote(half(idx, part), half(idx, part), send_sem.at[idx * 2 + part, way], recv_sem.at[idx, part], dev)
@@ -122,26 +120,32 @@
         return pltpu.make_async_copy(pre.at[plane_rows(zz), :], pre_out.at[plane_rows(zz), :], pre_sem.at[zz])
 
     def multiply(zz):
-        arrived(blk(1 - xpos, ypos, zz), 1)
-        arrived(blk(xpos, 1 - ypos, zz), 0)
-        arrived(blk(1 - xpos, 1 - ypos, zz), 0)
-        arrived(blk(1 - xpos, 1 - ypos, zz), 1)
+        for near_y in (True, False):
+            yy = ypos if near_y else 1 - ypos
+            if near_y:
+                arrived(blk(1 - xpos, ypos, zz), 1)
+            else:
+                arrived(blk(xpos, 1 - ypos, zz), 0)
+                arrived(blk(1 - xpos, 1 - ypos, zz), 0)
+                arrived(blk(1 - xpos, 1 - ypos, zz), 1)
+            here = pl.ds(pl.multiple_of((zz * 2 + yy) * 4 * rows, 4 * rows), 4 * rows)
+
+            def step(i, carry):
+                at = pl.ds(pl.multiple_of(i * CHUNK, CHUNK), CHUNK)
+                val = mm(buf[here, :], w_ref[:, at])
+                pre[here, at] = val
+                tot[:, at] += fold(val)
+                sqr[:, at] += fold(val * val)
+                return carry
+            lax.fori_loop(0, pre.shape[1] // CHUNK, step, 0)
         feat_copy(zz).start()
-
-        def step(i, carry):
-            at = pl.ds(pl.multiple_of(i * CHUNK, CHUNK), CHUNK)
-            val = mm(buf[plane_rows(zz), :], w_ref[:, at])
-            pre[plane_rows(zz), at] = val
-            tot[:, at] += fold(val)
-            sqr[:, at] += fold(val * val)
-            return carry
-        lax.fori_loop(0, pre.shape[1] // CHUNK, step, 0)
         pre_copy(zz).start()
 
-    for part in range(2):
-        column(zpos, part, True, True)
+    column(zpos, core, True, True)
     tot[...] = jnp.zeros_like(tot)
     sqr[...] = jnp.zeros_like(sqr)
+    remote(feat_a, half(chip, core), sib_s, sib_r, sib).wait()
+    column(zpos, 1 - core, True, True)
     load_w.wait()
 
     def level(dist, carry):
@@ -292,110 +296,36 @@
     return pltpu.make_async_copy(src.at[:, at_chunk(i)], dst.at[:, at_chunk(i)], sem.at[i])
 
 
-def schedule(tiles, chunks, load, begin, mul, fin, end):
-    j = pl.program_id(0)
-    zero = (jnp.zeros((8, TILE), F32),) * 2
-
-    @pl.when(j == 0)
-    def _():
-        for i in range(chunks):
-            load(i).start()
-        begin()
-
-        def step(i, sums):
-            load(i).wait()
-            return mul(i, sums)
-        end(lax.fori_loop(0, chunks, step, zero))
-
-    @pl.when(jnp.logical_and(j > 0, j < tiles))
-    def _():
-        begin()
-        sums = zero
-        for i in range(chunks):
-            fin(i)
-            sums = mul(i, sums)
-        end(sums)
-
-    @pl.when(j == tiles)
-    def _():
-        def step(i, carry):
-            fin(i)
-            return carry
-        lax.fori_loop(0, chunks, step, 0)
-
-
 def row_sum(val):
     return jnp.sum(val, axis=0, keepdims=True)
 
 
-def layer_kernel(tiles, x_hbm, w_ref, g_ref, b_ref, act_ref, norm_ref, inv_ref, x_ref, x_sem, pre, mean_s, inv_s):
+def share(hold, other_ref, send_sem, recv_sem, t):
+    return remote(hold.at[t], other_ref.at[:, at_tile(t)], send_sem.at[t], recv_sem.at[t], sibling_of(lax.axis_index(BATCH_AXIS)))
+
+
+def layers_kernel(tiles, x_hbm, w_ref, g_ref, b_ref, w_last, act_ref, pre_ref, mean_ref, inv_ref, emb_ref, norm_ref, inv_last, other_ref,
+                  x_ref, x_sem, act, pre, mean_s, inv_s, hold, send_sem, recv_sem):
     rows = x_ref.shape[0]
-
-    def mul(i, sums):
-        val = mm(x_ref[at_chunk(i), :], w_ref[...])
+    chunks = rows // CHUNK
+    step = pl.program_id(0)
+    j = step - tiles - 1
+    zero = (jnp.zeros((8, TILE), F32),) * 2
+
+    def mul(left, right, i, sums):
+        val = mm(left[at_chunk(i), :], right[...])
         pre[at_chunk(i), :] = val
         return sums[0] + fold(val), sums[1] + fold(val * val)
 
-    def fin(i):
-        norm = (pre[at_chunk(i), :] - mean_s[...]) * inv_s[...]
-        norm_ref[at_chunk(i), :] = norm
-        act_ref[at_chunk(i), :] = jnp.maximum(norm * g_ref[...] + b_ref[...], 0.0).astype(BF)
-
-    def end(sums):
-        mean = row_sum(sums[0]) / rows
-        mean_s[...] = mean
-        inv_s[...] = lax.rsqrt(row_sum(sums[1]) / rows - mean * mean + NORM_EPS)
-
-    @pl.when(pl.program_id(0) > 0)
-    def _():
-        inv_ref[...] = inv_s[...]
-    schedule(tiles, rows // CHUNK, functools.partial(row_load, x_hbm, x_ref, x_sem), lambda: None, mul, fin, end)
-
-
-def layer(x, w, gain, bias):
-    rows, width = x.shape[0], w.shape[1]
-    tiles = width // TILE
-    return pl.pallas_call(
-        functools.partial(layer_kernel, tiles), grid=(tiles + 1,),
-        out_shape=(jax.ShapeDtypeStruct((rows, width), BF), jax.ShapeDtypeStruct((rows, width), F32), jax.ShapeDtypeStruct((1, width), F32)),
-        in_specs=[any_spec(), col_now(w.shape[0], tiles), col_past(1), col_past(1)],
-        out_specs=(col_past(rows), col_past(rows), col_past(1)),
-        scratch_shapes=[pltpu.VMEM(x.shape, BF), pltpu.SemaphoreType.DMA((rows // CHUNK,)), pltpu.VMEM((rows, TILE), F32), pltpu.VMEM((1, TILE), F32), pltpu.VMEM((1, TILE), F32)],
-        compiler_params=params(), cost_estimate=cost(1), name='layer',
-    )(x, w, gain, bias)
-
-
-def share(hold, other_ref, send_sem, recv_sem, t):
-    return remote(hold.at[t], other_ref.at[:, at_tile(t)], send_sem.at[t], recv_sem.at[t], sibling_of(lax.axis_index(BATCH_AXIS)))
-
-
-def share_tiles(j, tiles, copy):
-    @pl.when(j > 0)
-    def _():
-        copy(j - 1).start()
-
-    @pl.when(j == tiles)
-    def _():
-        def last(t, carry):
-            copy(t).wait()
-            return carry
-        lax.fori_loop(0, tiles, last, 0)
-
-
-def embed_kernel(tiles, x_hbm, w_ref, emb_ref, norm_ref, inv_ref, other_ref, x_ref, x_sem, pre, mean_s, inv_s, hold, send_sem, recv_sem):
-    rows = x_ref.shape[0]
-    j = pl.program_id(0)
-
-    @pl.when(j == 0)
-    def _():
-        greet([sibling_of(lax.axis_index(BATCH_AXIS))])
-
-    def mul(i, sums):
-        val = mm(x_ref[at_chunk(i), :], w_ref[...])
-        pre[at_chunk(i), :] = val
-        return sums[0] + fold(val), sums[1] + fold(val * val)
-
-    def fin(i):
+    def fin_layer(i):
+        val = pre[at_chunk(i), :]
+        pre_ref[at_chunk(i), :] = val
+        norm = (val - mean_s[...]) * inv_s[...]
+        new = jnp.maximum(norm * g_ref[...] + b_ref[...], 0.0).astype(BF)
+        act_ref[at_chunk(i), :] = new
+        act[at_chunk(i), at_tile(jnp.clip(step - 1, 0, tiles - 1))] = new
+
+    def fin_last(i):
         norm = (pre[at_chunk(i), :] - mean_s[...]) * inv_s[...]
         norm_ref[at_chunk(i), :] = norm
         emb = norm.astype(BF)
@@ -407,31 +337,92 @@
         mean_s[...] = mean
         inv_s[...] = lax.rsqrt(row_sum(sums[1]) / rows - mean * mean + NORM_EPS)
 
+    @pl.when(step == 0)
+    def _():
+        for i in range(chunks):
+            row_load(x_hbm, x_ref, x_sem, i).start()
+        greet([sibling_of(lax.axis_index(BATCH_AXIS))])
+
+        def first(i, sums):
+            row_load(x_hbm, x_ref, x_sem, i).wait()
+            return mul(x_ref, w_ref, i, sums)
+        end(lax.fori_loop(0, chunks, first, zero))
+
+    @pl.when(jnp.logical_and(step > 0, step <= tiles))
+    def _():
+        mean_ref[...] = mean_s[...]
+        inv_ref[...] = inv_s[...]
+
     @pl.when(j > 0)
     def _():
-        inv_ref[...] = inv_s[...]
-    schedule(tiles, rows // CHUNK, functools.partial(row_load, x_hbm, x_ref, x_sem), lambda: None, mul, fin, end)
-    share_tiles(j, tiles, functools.partial(share, hold, other_ref, send_sem, recv_sem))
-
-
-def share_scratch(rows, tiles):
-    return [pltpu.VMEM((tiles, rows, TILE), BF), pltpu.SemaphoreType.DMA((tiles,)), pltpu.SemaphoreType.DMA((tiles,))]
-
-
-def embed(x, w):
+        inv_last[...] = inv_s[...]
+
+    def both(fin, left, right):
+        sums = zero
+        for i in range(chunks):
+            fin(i)
+            sums = mul(left, right, i, sums)
+        end(sums)
+
+    def only(fin):
+        def one(i, carry):
+            fin(i)
+            return carry
+        lax.fori_loop(0, chunks, one, 0)
+
+    @pl.when(jnp.logical_and(step > 0, step < tiles))
+    def _():
+        both(fin_layer, x_ref, w_ref)
+
+    @pl.when(step == tiles)
+    def _():
+        only(fin_layer)
+
+    @pl.when(j == 0)
+    def _():
+        end(lax.fori_loop(0, chunks, lambda i, sums: mul(act, w_last, i, sums), zero))
+
+    @pl.when(jnp.logical_and(j > 0, j < tiles))
+    def _():
+        both(fin_last, act, w_last)
+
+    @pl.when(j == tiles)
+    def _():
+        only(fin_last)
+    copy = functools.partial(share, hold, other_ref, send_sem, recv_sem)
+
+    @pl.when(j > 0)
+    def _():
+        copy(j - 1).start()
+
+    @pl.when(j == tiles)
+    def _():
+        def last(t, carry):
+            copy(t).wait()
+            return carry
+        lax.fori_loop(0, tiles, last, 0)
+
+
+def layers(x, w, gain, bias, w_last):
     rows, width = x.shape[0], w.shape[1]
     tiles = width // TILE
+    wide, tall, vec = jax.ShapeDtypeStruct((rows, width), BF), jax.ShapeDtypeStruct((rows, width), F32), jax.ShapeDtypeStruct((1, width), F32)
+    dma = pltpu.SemaphoreType.DMA
+
+    def col(height, first, offset):
+        return pl.BlockSpec((height, TILE), lambda s: (0, jnp.clip(s - first * (tiles + 1) - offset, 0, tiles - 1)))
     return pl.pallas_call(
-        functools.partial(embed_kernel, tiles), grid=(tiles + 1,),
-        out_shape=(jax.ShapeDtypeStruct((rows, width), BF), jax.ShapeDtypeStruct((rows, width), F32), jax.ShapeDtypeStruct((1, width), F32), jax.ShapeDtypeStruct((rows, width), BF)),
-        in_specs=[any_spec(), col_now(w.shape[0], tiles)],
-        out_specs=(col_past(rows), col_past(rows), col_past(1), any_spec()),
-        scratch_shapes=[pltpu.VMEM(x.shape, BF), pltpu.SemaphoreType.DMA((rows // CHUNK,)), pltpu.VMEM((rows, TILE), F32), pltpu.VMEM((1, TILE), F32), pltpu.VMEM((1, TILE), F32)] + share_scratch(rows, tiles),
-        compiler_params=params(collective_id=1, has_side_effects=True), cost_estimate=cost(1), name='embed',
-    )(x, w)
-
-
-def corr_kernel(lam_ref, emb_ref, other_ref, norm_ref, inv_ref, dout_ref, loss_ref, left, grad_c, scr):
+        functools.partial(layers_kernel, tiles), grid=(2 * tiles + 2,),
+        out_shape=(wide, tall, vec, vec, wide, tall, vec, wide),
+        in_specs=[any_spec(), col(w.shape[0], 0, 0), col(1, 0, 1), col(1, 0, 1), col(w_last.shape[0], 1, 0)],
+        out_specs=(col(rows, 0, 1), col(rows, 0, 1), col(1, 0, 1), col(1, 0, 1), col(rows, 1, 1), col(rows, 1, 1), col(1, 1, 1), any_spec()),
+        scratch_shapes=[pltpu.VMEM(x.shape, BF), dma((rows // CHUNK,)), pltpu.VMEM((rows, width), BF), pltpu.VMEM((rows, TILE), F32), pltpu.VMEM((1, TILE), F32), pltpu.VMEM((1, TILE), F32),
+                        pltpu.VMEM((tiles, rows, TILE), BF), dma((tiles,)), dma((tiles,))],
+        compiler_params=params(collective_id=1, has_side_effects=True), cost_estimate=cost(2), name='layers',
+    )(x, w, gain, bias, w_last)
+
+
+def corr_kernel(lam_ref, emb_ref, other_ref, norm_ref, inv_ref, dout_ref, loss_ref, grad_c, scr):
     j = pl.program_id(0)
     rows, width = other_ref.shape
     scale = 1.0 / rows
@@ -440,11 +431,10 @@
     @pl.when(j == 0)
     def _():
         loss_ref[...] = jnp.zeros_like(loss_ref)
-    left[...] = emb_ref[...].T
 
     def corr_step(i, loss):
         at = pl.ds(pl.multiple_of(i * CHUNK, CHUNK), CHUNK)
-        corr = mm(left[...], other_ref[:, at]) * scale
+        corr = mm(emb_ref[...], other_ref[:, at], 0, 0) * scale
         row_id = lax.broadcasted_iota(jnp.int32, corr.shape, 0) + j * TILE
         col_id = lax.broadcasted_iota(jnp.int32, corr.shape, 1) + i * CHUNK
         on_diag = row_id == col_id
@@ -480,7 +470,7 @@
         out_shape=(jax.ShapeDtypeStruct((rows, width), BF), jax.ShapeDtypeStruct((8, CHUNK), F32)),
         in_specs=[pl.BlockSpec(memory_space=pltpu.SMEM), col_same(rows), pl.BlockSpec(other.shape, lambda j: (0, 0), pipeline_mode=pl.Buffered(1)), col_same(rows), col_same(1)],
         out_specs=(col_same(rows), pl.BlockSpec((8, CHUNK), lambda j: (0, 0))),
-        scratch_shapes=[pltpu.VMEM((TILE, rows), BF), pltpu.VMEM((TILE, width), BF), pltpu.VMEM((rows, TILE), F32)],
+        scratch_shapes=[pltpu.VMEM((TILE, width), BF), pltpu.VMEM((rows, TILE), F32)],
         compiler_params=params(), cost_estimate=cost(2), name='corr_back',
     )(lam_off.reshape(1), emb, other, norm, inv)
 
@@ -490,8 +480,8 @@
         w_ref, pre_ref, mean_ref, scale_ref, inv_ref, g_ref, b_ref, g_old, dpre_ref, dg_ref, db_ref, dw_out = refs[:12]
         d_ref, d_sem, lhs, lhs_sem, sbuf, rbuf, ps, pr, os_, or_, ol, scr, norm_s, grad_s, cross_s = refs[12:]
     else:
-        small_ref, dw_out, small_out = refs[:3]
-        d_ref, d_sem, lhs, lhs_sem, sbuf, rbuf, ps, pr, os_, or_, ol, small_in, ss, sr = refs[3:]
+        vecs, loss_ref, dw_out, small_out = refs[:4], refs[4], refs[5], refs[6]
+        d_ref, d_sem, lhs, lhs_sem, sbuf, rbuf, ps, pr, os_, or_, ol, small_ref, small_in, ss, sr = refs[7:]
     step = pl.program_id(0)
     rows, width = d_ref.shape
     half = sbuf.shape[0]
@@ -541,7 +531,10 @@
         load_left(1).start()
         greet([sib])
         if not layered:
-            remote(small_ref, small_in, ss, sr, sib).start()
+            small_ref[...] = jnp.zeros_like(small_ref)
+            for k, vec in enumerate(vecs):
+                small_ref[k:k + 1, :] = vec[...]
+            small_ref[4:5, :] = jnp.zeros((1, width), F32) + jnp.where(core == 0, jnp.sum(loss_ref[...]), 0.0)
         load_left(0).wait()
 
         def first(i, carry):
@@ -558,6 +551,10 @@
         for i in range(chunks):
             sbuf[step, :, at_chunk(i)] = product(step, i)
         part_copy(step).start()
+        if not layered:
+            @pl.when(step == 1)
+            def _():
+                remote(small_ref, small_in, ss, sr, sib).start()
 
     if layered:
         def mul(i, sums):
@@ -648,12 +645,11 @@
         steps = 2 * half + tiles + 1
     else:
         tiles = 0
-        one = pl.BlockSpec(small.shape, lambda s: (0, 0))
-        in_specs = [hbm, hbm, one]
-        out_specs = (hbm, one)
-        out_shape = (dw, jax.ShapeDtypeStruct(small.shape, F32))
-        scratch += [pltpu.VMEM(small.shape, F32), dma, dma]
-        args = (act, grad, small)
+        in_specs = [hbm, hbm] + [pl.BlockSpec(v.shape, lambda s: (0, 0)) for v in small]
+        out_specs = (hbm, pl.BlockSpec((8, width), lambda s: (0, 0)))
+        out_shape = (dw, jax.ShapeDtypeStruct((8, width), F32))
+        scratch += [pltpu.VMEM((8, width), F32), pltpu.VMEM((8, width), F32), dma, dma]
+        args = (act, grad, *small)
         steps = 2 * half
     return pl.pallas_call(
         functools.partial(back_kernel, tiles, layer_args is not None), grid=(steps,),
@@ -666,18 +662,13 @@
     num_devs = mesh.shape[BATCH_AXIS]
 
     def local_step(feat_a, feat_b, w_one, w_two, w_three, g_one, b_one, g_two, b_two, lam_off):
-        first = lax.rem(lax.axis_index(BATCH_AXIS), 2) == 0
         g_one, b_one, g_two, b_two = (v.reshape(1, -1) for v in (g_one, b_one, g_two, b_two))
         feat, act_one, pre_one, mean_one, inv_one = gather_layer(feat_a, feat_b, w_one, g_one, b_one, num_devs)
-        act_two, norm_two, inv_two = layer(act_one, w_two, g_two, b_two)
-        emb, norm_out, inv_out, other = embed(act_two, w_three)
+        act_two, pre_two, mean_two, inv_two, emb, norm_out, inv_out, other = layers(act_one, w_two, g_two, b_two, w_three)
         grad_out, loss = corr_back(lam_off, emb, other, norm_out, inv_out)
-        loss_val = jnp.where(first, jnp.sum(loss), 0.0)
-        zero, one = jnp.zeros_like(g_two), jnp.ones_like(g_two)
-        grad_two, dg_two, db_two, dw_three = layer_back(2, act_two, grad_out, (w_three, norm_two, zero, one, inv_two, g_two, b_two))
+        grad_two, dg_two, db_two, dw_three = layer_back(2, act_two, grad_out, (w_three, pre_two, mean_two, inv_two, inv_two, g_two, b_two))
         grad_one, dg_one, db_one, dw_two = layer_back(3, act_one, grad_two, (w_two, pre_one, mean_one, inv_one, inv_one, g_one, b_one))
-        small = jnp.concatenate([dg_one, db_one, dg_two, db_two, zero + loss_val, zero, zero, zero])
-        dw_one, small = layer_back(4, feat, grad_one, small=small)
+        dw_one, small = layer_back(4, feat, grad_one, small=(dg_one, db_one, dg_two, db_two, loss))
         return (small[4, 0], dw_one, dw_two, dw_three, small[0], small[1], small[2], small[3])
 
     row_spec = P(BATCH_AXIS, None)

time: 374 us -> 364 us (0.973)
  Pallas kernels: 332 us -> 326 us
    pallas_call x2 -> x1, Pallas kernels: 57.1 us -> 55.3 us  [layers(): pl.pallas_call(functools.partial(layers_kernel, tiles), grid=(2 * tiles +...]
    unnamed x19 -> x13, local copies, waits for them, and re-layouts: 33.7 us -> 33.7 us
where the time goes in v3:
time: 364 us
  Pallas kernels  326 us (90%)
  local copies, waits for them, and re-layouts  36.5 us (10%)
    pallas_call x3, Pallas kernels, layer_back(): pl.pallas_call(functools.partial(back_kernel, tiles, layer_args is not No...  138 us
    pallas_call x1, Pallas kernels, gather_layer(): pl.pallas_call(functools.partial(gather_kernel, rows), out_shape=(jax.Sha...  86.7 us
    pallas_call x1, Pallas kernels, layers(): pl.pallas_call(functools.partial(layers_kernel, tiles), grid=(2 * tiles +...  55.3 us
    pallas_call x1, Pallas kernels, corr_back(): pl.pallas_call(corr_kernel, grid=(width // TILE,), out_shape=(jax.ShapeDt...  46.1 us
    unnamed x13, local copies, waits for them, and re-layouts  33.7 us

profile of v3, /device:TPU:0, one launch (start us, length us, event | category | flops | bytes accessed | tf_op | source)
XLA Modules:
  0.0 364.1 jit_solution(15842107958950050953)
XLA Ops:
  1.3 86.7 %gather_layer.1 = (bf16[2048,2048]{1,0:T(8,128)(2,1)}, bf16[2048,2048]{1,0:T(8,128)(2,1)}, f32[2048,2048]{1,0:T(8,128)}, f32[1,2048]{1,0:T(1,128)}, f32[1,2048]{1,0:T(1,128)}) custom-call(bf16[64,2048]{1,0:T(8,128)(2,1)} %feat_a.1, bf16[64,2048]{1,0:T(8,128)(2,1)} %feat_b.1, bf16[2048,2048]{1,0:T(8,128)(2,1)} %w_hbm.1, f32[1,2048]{1,0:T(1,128)} %bitcast.17, ...), custom_call_target="tpu_custom_call" | custom-call | tf_op jit(solution)/shard_map/gather_layer/pallas_call | solution.py:226
  88.0 55.3 %layers.1 = (bf16[2048,2048]{1,0:T(8,128)(2,1)}, f32[2048,2048]{1,0:T(8,128)}, f32[1,2048]{1,0:T(1,128)}, f32[1,2048]{1,0:T(1,128)}, bf16[2048,2048]{1,0:T(8,128...) custom-call(bf16[2048,2048]{1,0:T(8,128)(2,1)} %get-tuple-element.34.x_hbm.act_hbm, ...), custom_call_target="tpu_custom_call" | custom-call | flops 34359738368 | bytes 41943040 | tf_op jit(solution)/shard_map/layers/pallas_call | solution.py:414
  143.3 46.1 %corr_back.1 = (bf16[2048,2048]{1,0:T(8,128)(2,1)}, f32[8,512]{1,0:T(8,128)}) custom-call(f32[1]{0:T(128)} %bitcast.10.lam_ref, bf16[2048,2048]{1,0:T(8,128)(2,1)} %get-tuple-element.36.emb_ref, bf16[2048,2048]{1,0:T(8,128)(2,1)} %get-tuple-element.37.other_ref, f32[2048,2048]{1,0:T(8,128)} %get-tuple-element.38.norm_ref, f32[1,2048]{1,0:T(1,128)} %get-tuple-element.39.inv_ref), custom_call_target="tpu_custom_call" | custom-call | flops 34359738368 | bytes 41943040 | tf_op jit(solution)/shard_map/corr_back/pallas_call | solution.py:468
  189.4 52.9 %back_2.1 = (bf16[2048,2048]{1,0:T(8,128)(2,1)}, f32[1,2048]{1,0:T(1,128)}, f32[1,2048]{1,0:T(1,128)}, f32[2048,2048]{1,0:T(8,128)}) custom-call(bf16[2048,2048]{1,0:T(8,128)(2,1)} %get-tuple-element.35.act_hbm, bf16[2048,2048]{1,0:T(8,128)(2,1)} %get-tuple-element.40.d_hbm, bf16[2048,2048]{1,0:T(8,128)(2,1)} %refs_0_.2, ...), custom_call_target="tpu_custom_call" | custom-call | flops 34359738368 | bytes 41943040 | tf_op jit(solution)/shard_map/back_2/pallas_call | solution.py:654
  242.3 53.1 %back_3.1 = (bf16[2048,2048]{1,0:T(8,128)(2,1)}, f32[1,2048]{1,0:T(1,128)}, f32[1,2048]{1,0:T(1,128)}, f32[2048,2048]{1,0:T(8,128)}) custom-call(bf16[2048,2048]{1,0:T(8,128)(2,1)} %get-tuple-element.34.x_hbm.act_hbm, bf16[2048,2048]{1,0:T(8,128)(2,1)} %get-tuple-element.44.d_hbm, bf16[2048,2048]{1,0:T(8,128)(2,1)} %refs_0_.3, ...), custom_call_target="tpu_custom_call" | custom-call | flops 34359738368 | bytes 41943040 | tf_op jit(solution)/shard_map/back_3/pallas_call | solution.py:654
  295.4 32.2 %back_4.1 = (f32[2048,2048]{1,0:T(8,128)}, f32[8,2048]{1,0:T(8,128)}) custom-call(bf16[2048,2048]{1,0:T(8,128)(2,1)} %get-tuple-element.33.act_hbm, bf16[2048,2048]{1,0:T(8,128)(2,1)} %get-tuple-element.48.d_hbm, f32[1,2048]{1,0:T(1,128)} %get-tuple-element.49.refs_0_, f32[1,2048]{1,0:T(1,128)} %get-tuple-element.50.refs_1_, ...), custom_call_target="tpu_custom_call" | custom-call | flops 34359738368 | bytes 41943040 | tf_op jit(solution)/shard_map/back_4/pallas_call | solution.py:654
  327.6 1.2 slice.15
  328.8 1.6 fusion
  330.4 0.0 copy-start
  330.4 0.0 slice-start
  330.4 0.0 slice-start.1
  330.4 13.5 %copy.22 = f32[2048,2048]{1,0:T(8,128)} copy(f32[2048,2048]{1,0:T(8,128)} %get-tuple-element.71) | data formatting | bytes 33554432
  343.9 2.9 copy-done
  346.8 0.0 slice-start.2
  346.8 0.0 slice-start.3
  346.8 8.5 %copy.23 = f32[2048,2048]{1,0:T(8,128)} copy(f32[2048,2048]{1,0:T(8,128)S(1)} %copy-done) | data formatting | bytes 33554432
  355.3 0.0 slice-done
  355.3 0.0 slice-done.1
  355.3 1.4 slice-done.2
  356.7 1.2 slice-done.3
  357.9 6.2 %copy.24 = f32[2048,2048]{1,0:T(8,128)} copy(f32[2048,2048]{1,0:T(8,128)S(1)} %bitcast.12) | data formatting | bytes 33554432
  (1 shorter events, 0.0 us)
Async XLA Ops:
  330.4 16.4 %copy-start = (f32[2048,2048]{1,0:T(8,128)S(1)}, f32[2048,2048]{1,0:T(8,128)}, u32[]{:S(2)}) copy-start(f32[2048,2048]{1,0:T(8,128)} %get-tuple-element.72) | copy-start | bytes 50331652
  330.4 24.9 %slice-start = ((s8[16777216]{0:T(1024)(128)(4,1)}), s8[4194304]{0:T(1024)(128)(4,1)S(1)}, s32[]{:S(2)}) async-start(s8[16777216]{0:T(1024)(128)(4,1)} %bitcast.11), calls=%async_computation | async-start | bytes 8388608
  330.4 24.9 %slice-start.1 = ((s8[16777216]{0:T(1024)(128)(4,1)}), s8[4194304]{0:T(1024)(128)(4,1)S(1)}, s32[]{:S(2)}) async-start(s8[16777216]{0:T(1024)(128)(4,1)} %bitcast.11), calls=%async_computation.1 | async-start | bytes 8388608
  346.8 9.9 %slice-start.2 = ((s8[16777216]{0:T(1024)(128)(4,1)}), s8[4194304]{0:T(1024)(128)(4,1)S(1)}, s32[]{:S(2)}) async-start(s8[16777216]{0:T(1024)(128)(4,1)} %bitcast.11), calls=%async_computation.2 | async-start | bytes 8388608
  346.8 11.1 %slice-start.3 = ((s8[16777216]{0:T(1024)(128)(4,1)}), s8[4194304]{0:T(1024)(128)(4,1)S(1)}, s32[]{:S(2)}) async-start(s8[16777216]{0:T(1024)(128)(4,1)} %bitcast.11), calls=%async_computation.3 | async-start | bytes 8388608
